TPU v7x, 32 devices: a whole 2x2x4 slice. The times are simulated.
32 devices in a mesh: dp: 16 (over z, x, core), tensor: 2 (over y).
Axes of the slice: x: 2, y: 2, z: 4, core: 2. Of those that a mesh axis runs over, the one named last changes fastest.
Arguments:
- hidden_in: float32 [2816, 2048], P('dp'), may hold values from -6 to 6
- segment_ids: int32 [16, 176], P('dp'), may hold values from 0 to 5, never falling along the last dimension, each value on 1 to 96 neighbouring positions
- gain_attn: bfloat16 [1, 2048], P(None, 'dp'), may hold values from 0.5 to 1.5
- w_query: bfloat16 [1, 2048, 2048], P(None, 'dp', 'tensor'), may hold values from -0.125 to 0.125
- w_key: bfloat16 [1, 2048, 256], P(None, 'dp', 'tensor'), may hold values from -0.125 to 0.125
- w_value: bfloat16 [1, 2048, 256], P(None, 'dp', 'tensor'), may hold values from -0.125 to 0.125
- w_out: bfloat16 [1, 2048, 2048], P(None, 'tensor', 'dp'), may hold values from -0.4375 to 0.4375
- gain_ffn: bfloat16 [1, 2048], P(None, 'dp'), may hold values from 0.5 to 1.5
- w_gate: bfloat16 [1, 2048, 5632], P(None, 'dp', 'tensor'), may hold values from -0.125 to 0.125
- w_up: bfloat16 [1, 2048, 5632], P(None, 'dp', 'tensor'), may hold values from -0.125 to 0.125
- w_down: bfloat16 [1, 5632, 2048], P(None, 'tensor', 'dp'), may hold values from -0.078125 to 0.078125
- cotangent: float32 [2816, 2048], P('dp'), may hold values from -6 to 6
Outputs:
- hidden_out: float32 [2816, 2048], P('dp')
- grad_in: float32 [2816, 2048], P('dp')
- grad_gain_attn: float32 [1, 2048], P(None, 'dp')
- grad_w_query: float32 [1, 2048, 2048], P(None, 'dp', 'tensor')
- grad_w_key: float32 [1, 2048, 256], P(None, 'dp', 'tensor')
- grad_w_value: float32 [1, 2048, 256], P(None, 'dp', 'tensor')
- grad_w_out: float32 [1, 2048, 2048], P(None, 'tensor', 'dp')
- grad_gain_ffn: float32 [1, 2048], P(None, 'dp')
- grad_w_gate: float32 [1, 2048, 5632], P(None, 'dp', 'tensor')
- grad_w_up: float32 [1, 2048, 5632], P(None, 'dp', 'tensor')
- grad_w_down: float32 [1, 5632, 2048], P(None, 'tensor', 'dp')
Inputs may be any that keep to these rules, and one draw needn't show every extreme that they name: `segment_ids`: along a row of 176 tokens the ids never fall; a segment holds 1 to 96 tokens.
All inputs are finite; a program needn't handle non-finite values.
Results may differ from a plain program's by a relative error of at most 0.014.
Values may be sent and summed in bfloat16 or wider, within the bound.
A program may use at most 256 MiB of HBM per device.

v0:
```python
import jax
import jax.numpy as jnp
from jax import lax
from jax.sharding import PartitionSpec as P

HD = 64


epsilon = 1e-05
rope_base = 10000.0
masked_score = -1e30


def segment_positions(segment_ids):
    row_count, seq_len = segment_ids.shape
    index_grid = lax.broadcasted_iota(jnp.int32, (row_count, seq_len), 1)
    previous = jnp.concatenate([segment_ids[:, :1] - 1, segment_ids[:, :-1]], axis=1)
    starts = jnp.where(segment_ids != previous, index_grid, 0)
    return index_grid - lax.cummax(starts, axis=1)


def rope_tables(positions):
    half_dim = HD // 2
    inv_freq = rope_base ** (-(jnp.arange(half_dim, dtype=jnp.float32) * 2.0 / HD))
    angles = positions.astype(jnp.float32)[:, :, None] * inv_freq
    return (jnp.cos(angles), jnp.sin(angles))


def expand_table(table, values):
    extra_dims = values.ndim - 3
    return table.reshape(table.shape[:2] + (1,) * extra_dims + table.shape[2:])


def rotate_pairs(values, cos_t, sin_t):
    half_dim = values.shape[-1] // 2
    cos_e = expand_table(cos_t, values)
    sin_e = expand_table(sin_t, values)
    first, second = (values[..., :half_dim], values[..., half_dim:])
    return jnp.concatenate(
        [first * cos_e - second * sin_e, second * cos_e + first * sin_e], axis=-1
    )


def unrotate_pairs(values, cos_t, sin_t):
    half_dim = values.shape[-1] // 2
    cos_e = expand_table(cos_t, values)
    sin_e = expand_table(sin_t, values)
    first, second = (values[..., :half_dim], values[..., half_dim:])
    return jnp.concatenate(
        [first * cos_e + second * sin_e, second * cos_e - first * sin_e], axis=-1
    )


def attention_mask(segment_ids):
    seq_len = segment_ids.shape[1]
    same_seg = segment_ids[:, :, None] == segment_ids[:, None, :]
    query_pos = lax.broadcasted_iota(jnp.int32, (seq_len, seq_len), 0)
    key_pos = lax.broadcasted_iota(jnp.int32, (seq_len, seq_len), 1)
    return (same_seg & (key_pos <= query_pos))[:, None, None, :, :]


def score_block(query_heads, key_heads, allowed):
    scores = jnp.einsum(
        "rikgd,rjkd->rkgij", query_heads, key_heads, preferred_element_type=jnp.float32
    ) * HD ** (-0.5)
    return jnp.where(allowed, scores, masked_score)


def attend(query_heads, key_heads, value_heads, allowed):
    scores = score_block(query_heads, key_heads, allowed)
    row_max = jnp.max(scores, axis=-1, keepdims=True)
    log_norm = row_max + jnp.log(jnp.sum(jnp.exp(scores - row_max), axis=-1, keepdims=True))
    attn_probs = jnp.exp(scores - log_norm).astype(jnp.bfloat16)
    context = jnp.einsum(
        "rkgij,rjkd->rikgd", attn_probs, value_heads, preferred_element_type=jnp.float32
    )
    return (context.astype(jnp.bfloat16), log_norm)


def attend_back(query_heads, key_heads, value_heads, context, log_norm, grad_context, allowed):
    scores = score_block(query_heads, key_heads, allowed)
    probs_full = jnp.exp(scores - log_norm)
    probs_b = probs_full.astype(jnp.bfloat16)
    grad_v = jnp.einsum(
        "rkgij,rikgd->rjkd", probs_b, grad_context, preferred_element_type=jnp.float32
    )
    grad_probs = jnp.einsum(
        "rikgd,rjkd->rkgij", grad_context, value_heads, preferred_element_type=jnp.float32
    )
    delta = jnp.sum(grad_context.astype(jnp.float32) * context.astype(jnp.float32), axis=-1)
    delta = jnp.transpose(delta, (0, 2, 3, 1))[..., None]
    grad_scores = (probs_full * (grad_probs - delta)).astype(jnp.bfloat16)
    grad_q = jnp.einsum(
        "rkgij,rjkd->rikgd", grad_scores, key_heads, preferred_element_type=jnp.float32
    ) * HD ** (-0.5)
    grad_k = jnp.einsum(
        "rkgij,rikgd->rjkd", grad_scores, query_heads, preferred_element_type=jnp.float32
    ) * HD ** (-0.5)
    return (grad_q, grad_k, grad_v)


def contract_rows(left, right):
    return lax.dot_general(
        left, right, (((0,), (0,)), ((), ())), preferred_element_type=jnp.float32
    )


def contract_cols(left, right):
    return lax.dot_general(
        left, right, (((1,), (1,)), ((), ())), preferred_element_type=jnp.float32
    )


def norm_backward(resid, recip, gain, grad_normed):
    scaled = grad_normed * gain.astype(jnp.float32)
    grad_gain = jnp.sum(grad_normed * resid * recip, axis=0)
    grad_resid = recip * scaled - resid * (recip * recip * recip) * jnp.mean(
        scaled * resid, axis=-1, keepdims=True
    )
    return (grad_gain, grad_resid)


def layer_forward(resid, weights, cos_t, sin_t, allowed):
    gain_one, w_query, w_key, w_value, w_out, gain_two, w_gate, w_up, w_down = weights
    row_count, seq_len = (cos_t.shape[0], cos_t.shape[1])
    heads_here = w_query.shape[1] // HD
    kv_here = w_key.shape[1] // HD
    group_size = heads_here // kv_here
    recip_one = lax.rsqrt(jnp.mean(resid * resid, axis=-1, keepdims=True) + epsilon)
    normed_one = (resid * recip_one * gain_one.astype(jnp.float32)).astype(jnp.bfloat16)
    query_raw = jnp.dot(normed_one, w_query, preferred_element_type=jnp.float32)
    query_heads = rotate_pairs(
        query_raw.reshape(row_count, seq_len, kv_here, group_size, HD), cos_t, sin_t
    ).astype(jnp.bfloat16)
    key_raw = jnp.dot(normed_one, w_key, preferred_element_type=jnp.float32)
    key_heads = rotate_pairs(key_raw.reshape(row_count, seq_len, kv_here, HD), cos_t, sin_t).astype(
        jnp.bfloat16
    )
    value_raw = jnp.dot(normed_one, w_value, preferred_element_type=jnp.float32)
    value_heads = value_raw.reshape(row_count, seq_len, kv_here, HD).astype(jnp.bfloat16)
    context, log_norm = attend(query_heads, key_heads, value_heads, allowed)
    context_flat = context.reshape(row_count * seq_len, heads_here * HD)
    attn_sum = lax.psum(jnp.dot(context_flat, w_out, preferred_element_type=jnp.float32), "tensor")
    middle = resid + attn_sum
    recip_two = lax.rsqrt(jnp.mean(middle * middle, axis=-1, keepdims=True) + epsilon)
    normed_two = (middle * recip_two * gain_two.astype(jnp.float32)).astype(jnp.bfloat16)
    gate = jnp.dot(normed_two, w_gate, preferred_element_type=jnp.float32)
    up_proj = jnp.dot(normed_two, w_up, preferred_element_type=jnp.float32)
    hidden_act = (jax.nn.silu(gate) * up_proj).astype(jnp.bfloat16)
    feed_out = lax.psum(jnp.dot(hidden_act, w_down, preferred_element_type=jnp.float32), "tensor")
    kept_state = (
        resid,
        recip_one,
        normed_one,
        query_heads,
        key_heads,
        value_heads,
        context,
        log_norm,
        middle,
        recip_two,
        normed_two,
        gate,
        up_proj,
        hidden_act,
    )
    return (middle + feed_out, kept_state)


def backward_layer(grad_resid, kept_state, weights, cos_t, sin_t, allowed):
    (
        resid,
        recip_one,
        normed_one,
        query_heads,
        key_heads,
        value_heads,
        context,
        log_norm,
        middle,
        recip_two,
        normed_two,
        gate,
        up_proj,
        hidden_act,
    ) = kept_state
    gain_one, w_query, w_key, w_value, w_out, gain_two, w_gate, w_up, w_down = weights
    token_count = resid.shape[0]
    grad_b = grad_resid.astype(jnp.bfloat16)
    grad_down = contract_rows(hidden_act, grad_b)
    grad_hidden = contract_cols(grad_b, w_down)
    sigma = jax.nn.sigmoid(gate)
    grad_gate_b = (grad_hidden * up_proj * sigma * (1.0 + gate * (1.0 - sigma))).astype(
        jnp.bfloat16
    )
    grad_up_b = (grad_hidden * (gate * sigma)).astype(jnp.bfloat16)
    grad_gate_w = contract_rows(normed_two, grad_gate_b)
    grad_up_w = contract_rows(normed_two, grad_up_b)
    grad_normed_two = lax.psum(
        contract_cols(grad_gate_b, w_gate) + contract_cols(grad_up_b, w_up), "tensor"
    )
    grad_gain_two, grad_mid_norm = norm_backward(middle, recip_two, gain_two, grad_normed_two)
    grad_middle = grad_resid + grad_mid_norm
    middle_b = grad_middle.astype(jnp.bfloat16)
    context_flat = context.reshape(token_count, -1)
    grad_out_w = contract_rows(context_flat, middle_b)
    grad_context = contract_cols(middle_b, w_out).astype(jnp.bfloat16).reshape(context.shape)
    grad_q, grad_k, grad_v = attend_back(
        query_heads, key_heads, value_heads, context, log_norm, grad_context, allowed
    )
    grad_q = unrotate_pairs(grad_q, cos_t, sin_t).astype(jnp.bfloat16).reshape(token_count, -1)
    grad_k = unrotate_pairs(grad_k, cos_t, sin_t).astype(jnp.bfloat16).reshape(token_count, -1)
    grad_v = grad_v.astype(jnp.bfloat16).reshape(token_count, -1)
    grad_query_w = contract_rows(normed_one, grad_q)
    grad_key_w = contract_rows(normed_one, grad_k)
    grad_value_w = contract_rows(normed_one, grad_v)
    grad_normed_one = lax.psum(
        contract_cols(grad_q, w_query)
        + contract_cols(grad_k, w_key)
        + contract_cols(grad_v, w_value),
        "tensor",
    )
    grad_gain_one, grad_res_norm = norm_backward(resid, recip_one, gain_one, grad_normed_one)
    grad_input = grad_middle + grad_res_norm
    layer_grads = (
        lax.psum_scatter(grad_gain_one, "dp", scatter_dimension=0, tiled=True),
        lax.psum_scatter(grad_query_w, "dp", scatter_dimension=0, tiled=True),
        lax.psum_scatter(grad_key_w, "dp", scatter_dimension=0, tiled=True),
        lax.psum_scatter(grad_value_w, "dp", scatter_dimension=0, tiled=True),
        lax.psum_scatter(grad_out_w, "dp", scatter_dimension=1, tiled=True),
        lax.psum_scatter(grad_gain_two, "dp", scatter_dimension=0, tiled=True),
        lax.psum_scatter(grad_gate_w, "dp", scatter_dimension=0, tiled=True),
        lax.psum_scatter(grad_up_w, "dp", scatter_dimension=0, tiled=True),
        lax.psum_scatter(grad_down, "dp", scatter_dimension=1, tiled=True),
    )
    return (grad_input, tuple(layer_grads))


def body(
    hidden_in,
    segment_ids,
    gain_attn,
    w_query,
    w_key,
    w_value,
    w_out,
    gain_ffn,
    w_gate,
    w_up,
    w_down,
    cotangent,
):
    cos_t, sin_t = rope_tables(segment_positions(segment_ids))
    allowed = attention_mask(segment_ids)
    layer_count = w_query.shape[0]
    resid = hidden_in
    retained = []
    layer_no = 0
    gathered = (
        lax.all_gather(gain_attn[layer_no], "dp", axis=0, tiled=True),
        lax.all_gather(w_query[layer_no], "dp", axis=0, tiled=True),
        lax.all_gather(w_key[layer_no], "dp", axis=0, tiled=True),
        lax.all_gather(w_value[layer_no], "dp", axis=0, tiled=True),
        lax.all_gather(w_out[layer_no], "dp", axis=1, tiled=True),
        lax.all_gather(gain_ffn[layer_no], "dp", axis=0, tiled=True),
        lax.all_gather(w_gate[layer_no], "dp", axis=0, tiled=True),
        lax.all_gather(w_up[layer_no], "dp", axis=0, tiled=True),
        lax.all_gather(w_down[layer_no], "dp", axis=1, tiled=True),
    )
    retained.append(gathered)
    resid, kept_state = layer_forward(resid, gathered, cos_t, sin_t, allowed)
    states = [kept_state]
    grad_resid = cotangent
    collected = [None] * layer_count
    for layer_no in reversed(range(layer_count)):
        gathered = (
            lax.all_gather(gain_attn[layer_no], "dp", axis=0, tiled=True),
            lax.all_gather(w_query[layer_no], "dp", axis=0, tiled=True),
            lax.all_gather(w_key[layer_no], "dp", axis=0, tiled=True),
            lax.all_gather(w_value[layer_no], "dp", axis=0, tiled=True),
            lax.all_gather(w_out[layer_no], "dp", axis=1, tiled=True),
            lax.all_gather(gain_ffn[layer_no], "dp", axis=0, tiled=True),
            lax.all_gather(w_gate[layer_no], "dp", axis=0, tiled=True),
            lax.all_gather(w_up[layer_no], "dp", axis=0, tiled=True),
            lax.all_gather(w_down[layer_no], "dp", axis=1, tiled=True),
        )
        grad_resid, collected[layer_no] = backward_layer(
            grad_resid, states[layer_no], gathered, cos_t, sin_t, allowed
        )
    stacked = tuple((jnp.stack([collected[0][member]]) for member in range(9)))
    return (
        resid,
        grad_resid,
        stacked[0],
        stacked[1],
        stacked[2],
        stacked[3],
        stacked[4],
        stacked[5],
        stacked[6],
        stacked[7],
        stacked[8],
    )


def solution(mesh):
    return jax.shard_map(
        body,
        mesh=mesh,
        in_specs=(
            P("dp", None),
            P("dp", None),
            P(None, "dp"),
            P(None, "dp", "tensor"),
            P(None, "dp", "tensor"),
            P(None, "dp", "tensor"),
            P(None, "tensor", "dp"),
            P(None, "dp"),
            P(None, "dp", "tensor"),
            P(None, "dp", "tensor"),
            P(None, "tensor", "dp"),
            P("dp", None),
        ),
        out_specs=(
            P("dp", None),
            P("dp", None),
            P(None, "dp"),
            P(None, "dp", "tensor"),
            P(None, "dp", "tensor"),
            P(None, "dp", "tensor"),
            P(None, "tensor", "dp"),
            P(None, "dp"),
            P(None, "dp", "tensor"),
            P(None, "dp", "tensor"),
            P(None, "tensor", "dp"),
        ),
        check_vma=False,
    )
```

profile of v0, /device:TPU:0, one launch (start us, length us, event | category | flops | bytes accessed | tf_op | source)
XLA Modules:
  0.0 1672.7 jit_solution(2110594264487035066)
XLA Ops:
  7.2 0.7 all-gather.15.cloned.1.call-update
  8.0 0.7 all-gather.17.cloned.1.call-update
  8.7 23.3 %all-gather = bf16[1,2048]{1,0:T(2,128)(2,1)S(1)} all-gather(bf16[1,128]{1,0:T(2,128)(2,1)} %param.14), channel_id=2, replica_groups=mesh['dp'=16,'tensor'=2] {'dp'}, dimensions={1}, use_global_device_ids=true | all-gather | bytes 4352 | tf_op jit(solution)/shard_map/all_gather | solution.py:260
  32.0 1.5 multiply_reduce_fusion.5
  33.6 0.6 multiply_multiply_fusion
  34.2 20.6 %all-gather.1 = bf16[1,2048,128]{2,1,0:T(8,128)(2,1)S(1)} all-gather(bf16[1,128,128]{2,1,0:T(8,128)(2,1)S(1)} %copy-done.32), channel_id=3, replica_groups=mesh['dp'=16,'tensor'=2] {'dp'}, dimensions={1}, use_global_device_ids=true | all-gather | bytes 557056 | tf_op jit(solution)/shard_map/all_gather | solution.py:263
  55.0 0.6 copy-done.10
  58.4 21.7 %all-gather.2 = bf16[1,2048,128]{2,1,0:T(8,128)(2,1)S(1)} all-gather(bf16[1,128,128]{2,1,0:T(8,128)(2,1)S(1)} %copy-done.33), channel_id=4, replica_groups=mesh['dp'=16,'tensor'=2] {'dp'}, dimensions={1}, use_global_device_ids=true | all-gather | bytes 557056 | tf_op jit(solution)/shard_map/all_gather | solution.py:262
  80.2 0.8 copy-done.12
  81.5 3.9 fusion.18
  85.6 0.7 fusion.30
  86.4 0.7 exponential_reduce_fusion
  87.1 0.8 copy-done.16
  88.0 0.8 convolution_convert_fusion
  88.8 31.8 %all-gather.17.cloned.1.call-done = bf16[1,1024,2048]{2,1,0:T(8,128)(2,1)} async-done(((bf16[1,1024,128]{2,1,0:T(8,128)(2,1)}), bf16[1,1024,2048]{2,1,0:T(8,128)(2,1)}) %all-gather.17.cloned.1.call-update) | async-done | bytes 4194320 | tf_op jit(solution)/shard_map/all_gather | solution.py:264
  120.6 4.2 fusion.14
  126.6 18.7 %all-gather.5 = bf16[1,2048]{1,0:T(2,128)(2,1)S(1)} all-gather(bf16[1,128]{1,0:T(2,128)(2,1)S(1)} %copy-done.40), channel_id=7, replica_groups=mesh['dp'=16,'tensor'=2] {'dp'}, dimensions={1}, use_global_device_ids=true | all-gather | bytes 4352 | tf_op jit(solution)/shard_map/all_gather | solution.py:265
  145.4 26.5 %all-reduce.9.cloned.1.call-done = f32[176,2048]{1,0:T(8,128)} async-done(((f32[176,2048]{1,0:T(8,128)}), f32[176,2048]{1,0:T(8,128)}) %all-reduce.9.cloned.1.call-update) | async-done | bytes 1441808 | tf_op jit(solution)/shard_map/psum | solution.py:143
  171.8 1.6 multiply_reduce_fusion.4
  173.4 1.1 multiply_convert_fusion.3
  174.5 93.5 %all-gather.21.cloned.1.call-done = bf16[1,2048,2816]{2,1,0:T(8,128)(2,1)} async-done(((bf16[1,128,2816]{2,1,0:T(8,128)(2,1)}), bf16[1,2048,2816]{2,1,0:T(8,128)(2,1)}) %all-gather.21.cloned.1.call-update) | async-done | bytes 11534352 | tf_op jit(solution)/shard_map/all_gather | solution.py:267
  268.0 8.0 fusion.6
  276.0 89.2 %all-gather.23.cloned.1.call-done = bf16[1,2816,2048]{2,1,0:T(8,128)(2,1)} async-done(((bf16[1,2816,128]{2,1,0:T(8,128)(2,1)}), bf16[1,2816,2048]{2,1,0:T(8,128)(2,1)}) %all-gather.23.cloned.1.call-update) | async-done | bytes 11534352 | tf_op jit(solution)/shard_map/all_gather | solution.py:268
  365.2 10.0 fusion
  375.2 84.3 %all-gather.19.cloned.1.call-done = bf16[1,2048,2816]{2,1,0:T(8,128)(2,1)} async-done(((bf16[1,128,2816]{2,1,0:T(8,128)(2,1)}), bf16[1,2048,2816]{2,1,0:T(8,128)(2,1)}) %all-gather.19.cloned.1.call-update) | async-done | bytes 11534352 | tf_op jit(solution)/shard_map/all_gather | solution.py:266
  459.5 9.4 multiply_convert_fusion.1
  468.9 8.9 fusion.4
  477.9 5.0 fusion.26
  483.2 8.4 fusion.2
  491.6 38.4 %all-reduce.11.cloned.1.call-done = f32[176,2048]{1,0:T(8,128)} async-done(((f32[176,2048]{1,0:T(8,128)}), f32[176,2048]{1,0:T(8,128)}) %all-reduce.11.cloned.1.call-update) | async-done | bytes 1441808 | tf_op jit(solution)/shard_map/psum | solution.py:199
  530.0 1.9 multiply_reduce_fusion
  532.6 1.1 copy-done.2
  533.8 1.1 copy-done.4
  534.9 2.3 fusion.34
  537.2 2.0 copy.49
  539.2 2.2 copy.50
  541.3 1.4 multiply_reduce_fusion.6
  542.9 2.8 fusion.31
  545.7 0.6 fusion.38
  546.7 0.8 copy-done.17
  547.5 0.8 fusion.39
  549.2 1.7 copy-done.14
  550.9 1.6 fusion.22
  552.5 1.5 convolution_add_fusion
  554.1 2.6 fusion.70
  556.8 2.6 fusion.71
  559.5 6.2 fusion.69
  566.0 6.0 fusion.46
  572.0 12.4 fusion.72
  584.5 12.4 fusion.73
  596.9 13.1 fusion.49
  610.1 0.6 copy-done.41
  610.7 0.6 dynamic-slice
  611.9 22.4 %all-reduce.13.cloned.1.call-done = (f32[176,2048]{1,0:T(8,128)}, f32[176,2048]{1,0:T(8,128)}) async-done(((f32[176,2048]{1,0:T(8,128)}, f32[176,2048]{1,0:T(8,128)}), (f32[176,2048]{1,0:T(8,128)}, f32[176,2048]{1,0:T(8,128)})) %all-reduce.13.cloned.1.call-update) | async-done | bytes 2883600 | tf_op jit(solution)/shard_map/psum | solution.py:150
  634.3 2.7 add.107
  637.5 61.0 %all-reduce.3 = (f32[2048]{0:T(1024)S(1)}, f32[2048]{0:T(1024)S(1)}) all-reduce(f32[2048]{0:T(1024)S(1)} %get-tuple-element.13, f32[2048]{0:T(1024)S(1)} %get-tuple-element.11), channel_id=11, replica_groups=mesh['dp'=16,'tensor'=2] {'dp'}, use_global_device_ids=true, to_apply=%region_14.15.clone | all-reduce | flops 4096 | bytes 32768
  698.5 0.6 dynamic-slice_bitcast_fusion
  699.1 2.9 subtract_add_fusion
  702.0 54.9 %reduce-scatter.12.cloned.1.call-done = f32[128,128]{1,0:T(8,128)} async-done(((f32[2048,128]{1,0:T(8,128)}), f32[128,128]{1,0:T(8,128)}) %reduce-scatter.12.cloned.1.call-update) | async-done | bytes 65552 | tf_op jit(solution)/shard_map/reduce_scatter | solution.py:229
  756.9 107.1 %reduce-scatter.8.cloned.1.call-done = f32[128,1024]{1,0:T(8,128)} async-done(((f32[2048,1024]{1,0:T(8,128)}), f32[128,1024]{1,0:T(8,128)}) %reduce-scatter.8.cloned.1.call-update) | async-done | bytes 524304 | tf_op jit(solution)/shard_map/reduce_scatter | solution.py:227
  864.0 107.7 %reduce-scatter.14.cloned.1.call-done = f32[1024,128]{1,0:T(8,128)} async-done(((f32[1024,2048]{1,0:T(8,128)}), f32[1024,128]{1,0:T(8,128)}) %reduce-scatter.14.cloned.1.call-update) | async-done | bytes 524304 | tf_op jit(solution)/shard_map/reduce_scatter | solution.py:230
  971.7 231.9 %reduce-scatter.16.cloned.1.call-done = f32[128,2816]{1,0:T(8,128)} async-done(((f32[2048,2816]{1,0:T(8,128)}), f32[128,2816]{1,0:T(8,128)}) %reduce-scatter.16.cloned.1.call-update) | async-done | bytes 1441808 | tf_op jit(solution)/shard_map/reduce_scatter | solution.py:232
  1203.6 231.2 %reduce-scatter.18.cloned.1.call-done = f32[128,2816]{1,0:T(8,128)} async-done(((f32[2048,2816]{1,0:T(8,128)}), f32[128,2816]{1,0:T(8,128)}) %reduce-scatter.18.cloned.1.call-update) | async-done | bytes 1441808 | tf_op jit(solution)/shard_map/reduce_scatter | solution.py:233
  1434.8 230.9 %reduce-scatter.20.cloned.1.call-done = f32[2816,128]{1,0:T(8,128)} async-done(((f32[2816,2048]{1,0:T(8,128)}), f32[2816,128]{1,0:T(8,128)}) %reduce-scatter.20.cloned.1.call-update) | async-done | bytes 1441808 | tf_op jit(solution)/shard_map/reduce_scatter | solution.py:234
  (138 shorter events, 8.5 us)
Async XLA Ops:
  7.2 47.6 %copy-start = (f32[176,2048]{1,0:T(8,128)S(1)}, f32[176,2048]{1,0:T(8,128)}, u32[]{:S(2)}) copy-start(f32[176,2048]{1,0:T(8,128)} %param.12) | copy-start | bytes 4325380
  7.2 27.0 %copy-start.32 = (bf16[1,128,128]{2,1,0:T(8,128)(2,1)S(1)}, bf16[1,128,128]{2,1,0:T(8,128)(2,1)}, u32[]{:S(2)}) copy-start(bf16[1,128,128]{2,1,0:T(8,128)(2,1)} %param.17) | copy-start | bytes 98308
  7.2 74.2 %all-gather.15.cloned.1.call-start = ((), (), s32[]{:S(2)}) async-start(), calls=%async_computation.16 | async-start | bytes 4456448 | tf_op jit(solution)/shard_map/all_gather | solution.py:261
  7.9 112.6 %all-gather.17.cloned.1.call-start = ((), (), s32[]{:S(2)}) async-start(), calls=%async_computation.17 | async-start | bytes 4456448 | tf_op jit(solution)/shard_map/all_gather | solution.py:264
  8.7 163.1 %all-reduce.9.cloned.1.call-start = ((), (), s32[]{:S(2)}) async-start(), calls=%async_computation.7 | async-start | bytes 2883584 | tf_op jit(solution)/shard_map/psum | solution.py:143
  34.2 20.6 %copy-start.34 = (f32[176]{0:T(256)}, f32[176]{0:T(256)S(1)}, u32[]{:S(2)}) copy-start(f32[176]{0:T(256)S(1)} %get-tuple-element.35) | copy-start | bytes 2116
  54.8 0.8 copy-start.10
  54.8 1.2 copy-start.38
  54.8 3.6 copy-start.33
  55.6 25.9 %copy-start.1 = (bf16[176,2048]{1,0:T(8,128)(2,1)}, bf16[176,2048]{1,0:T(8,128)(2,1)S(1)}, u32[]{:S(2)}) copy-start(bf16[176,2048]{1,0:T(8,128)(2,1)S(1)} %multiply_convert_fusion.4) | copy-start | bytes 2162692
  56.1 31.0 %copy-start.30 = (bf16[176,128]{0,1:T(8,128)(2,1)}, bf16[176,128]{0,1:T(8,128)(2,1)S(1)}, u32[]{:S(2)}) copy-start(bf16[176,128]{0,1:T(8,128)(2,1)S(1)} %copy.45) | copy-start | bytes 135172
  80.2 0.8 copy-start.12
  81.4 4.2 copy-start.26
  81.4 4.2 copy-start.28
  85.6 0.7 copy-start.18
  85.6 0.8 copy-start.20
  86.4 1.5 copy-start.16
  87.1 1.7 copy-start.36
  124.8 1.8 copy-start.40
  124.8 143.1 %all-gather.21.cloned.1.call-start = ((), (), s32[]{:S(2)}) async-start(), calls=%async_computation.19 | async-start | bytes 12255232 | tf_op jit(solution)/shard_map/all_gather | solution.py:267
  125.4 239.7 %all-gather.23.cloned.1.call-start = ((), (), s32[]{:S(2)}) async-start(), calls=%async_computation.20 | async-start | bytes 12255232 | tf_op jit(solution)/shard_map/all_gather | solution.py:268
  126.0 333.5 %all-gather.19.cloned.1.call-start = ((), (), s32[]{:S(2)}) async-start(), calls=%async_computation.18 | async-start | bytes 12255232 | tf_op jit(solution)/shard_map/all_gather | solution.py:266
  126.6 403.4 %all-reduce.11.cloned.1.call-start = ((), (), s32[]{:S(2)}) async-start(), calls=%async_computation.8 | async-start | bytes 2883584 | tf_op jit(solution)/shard_map/psum | solution.py:199
  468.9 8.9 copy-start.22
  468.9 8.9 copy-start.15
  468.9 8.9 copy-start.6
  482.9 151.4 %all-reduce.13.cloned.1.call-start = ((), (), s32[]{:S(2)}) async-start(), calls=%async_computation.21 | async-start | bytes 5767168 | tf_op jit(solution)/shard_map/psum | solution.py:150
  530.0 1.9 copy-start.5
  530.0 2.2 copy-start.8
  532.2 2.7 copy-start.4
  532.6 1.1 copy-start.2
  541.3 1.5 copy-start.23
  541.3 1.5 copy-start.31
  541.3 1.5 copy-start.37
  542.8 2.9 copy-start.19
  542.8 2.9 copy-start.21
  542.8 3.4 copy-start.27
  542.8 3.4 copy-start.29
  545.7 1.8 copy-start.17
  547.5 1.0 copy-start.13
  548.3 4.2 copy-start.24
  548.5 2.4 copy-start.14
  549.2 3.3 copy-start.9
  550.9 1.6 copy-start.11
  554.0 2.7 copy-start.25
  554.0 148.0 %reduce-scatter.10.cloned.1.call-start = ((), (), s32[]{:S(2)}) async-start(), calls=%async_computation.10 | async-start | bytes 1114112 | tf_op jit(solution)/shard_map/reduce_scatter | solution.py:228
  556.7 200.2 %reduce-scatter.12.cloned.1.call-start = ((), (), s32[]{:S(2)}) async-start(), calls=%async_computation.11 | async-start | bytes 1114112 | tf_op jit(solution)/shard_map/reduce_scatter | solution.py:229
  559.4 304.6 %reduce-scatter.8.cloned.1.call-start = ((), (), s32[]{:S(2)}) async-start(), calls=%async_computation.9 | async-start | bytes 8912896 | tf_op jit(solution)/shard_map/reduce_scatter | solution.py:227
  565.7 406.1 %reduce-scatter.14.cloned.1.call-start = ((), (), s32[]{:S(2)}) async-start(), calls=%async_computation.12 | async-start | bytes 8912896 | tf_op jit(solution)/shard_map/reduce_scatter | solution.py:230
  572.0 631.6 %reduce-scatter.16.cloned.1.call-start = ((), (), s32[]{:S(2)}) async-start(), calls=%async_computation.13 | async-start | bytes 24510464 | tf_op jit(solution)/shard_map/reduce_scatter | solution.py:232
  584.4 850.4 %reduce-scatter.18.cloned.1.call-start = ((), (), s32[]{:S(2)}) async-start(), calls=%async_computation.14 | async-start | bytes 24510464 | tf_op jit(solution)/shard_map/reduce_scatter | solution.py:233
  596.9 1068.8 %reduce-scatter.20.cloned.1.call-start = ((), (), s32[]{:S(2)}) async-start(), calls=%async_computation.15 | async-start | bytes 24510464 | tf_op jit(solution)/shard_map/reduce_scatter | solution.py:234
  610.0 0.7 copy-start.41
  634.3 2.7 copy-start.7
  634.3 2.7 copy-start.35
  637.0 62.1 %copy-start.3 = (f32[176,2048]{1,0:T(8,128)S(1)}, f32[176,2048]{1,0:T(8,128)}, u32[]{:S(2)}) copy-start(f32[176,2048]{1,0:T(8,128)} %copy-done.2) | copy-start | bytes 4325380
  637.0 62.1 %copy-start.39 = (f32[176]{0:T(256)S(1)}, f32[176]{0:T(256)}, u32[]{:S(2)}) copy-start(f32[176]{0:T(256)} %get-tuple-element.34) | copy-start | bytes 2116
Sparse Core Ops, SparseCore 0:
  10.2 55.8 all-gather.14
  68.2 52.2 all-gather.16
  124.9 46.8 all-reduce.8
  174.0 93.9 all-gather.20
  270.0 95.1 all-gather.22
  367.3 92.1 all-gather.18
  483.0 46.8 all-reduce.10
  554.1 80.0 all-reduce.12
  638.5 57.5 reduce-scatter.9
  700.1 56.6 reduce-scatter.11
  761.5 102.4 reduce-scatter.7
  868.5 103.1 reduce-scatter.13
  976.4 227.1 reduce-scatter.15
  1208.1 226.5 reduce-scatter.17
  1439.3 226.3 reduce-scatter.19
where the time goes:
time: 1680 us; the launch traced here: 1670 us
  waiting for transfers between devices  1350 us (80%)
  blocking collectives  145 us (9%)
  matrix products  126 us (8%)
  other arithmetic  16.9 us (1%)
    reduce_scatter x1, waiting for transfers between devices, backward_layer(): lax.psum_scatter(grad_gate_w, 'dp', scatter_dimension=0, tiled=True)  232 us
    reduce_scatter x1, waiting for transfers between devices, backward_layer(): lax.psum_scatter(grad_up_w, 'dp', scatter_dimension=0, tiled=True)  231 us
    reduce_scatter x1, waiting for transfers between devices, backward_layer(): lax.psum_scatter(grad_down, 'dp', scatter_dimension=1, tiled=True)  231 us
    reduce_scatter x1, waiting for transfers between devices, backward_layer(): lax.psum_scatter(grad_out_w, 'dp', scatter_dimension=1, tiled=True)  108 us
    reduce_scatter x1, waiting for transfers between devices, backward_layer(): lax.psum_scatter(grad_query_w, 'dp', scatter_dimension=0, tiled=True)  107 us
    all_gather x1, waiting for transfers between devices, body(): lax.all_gather(w_up[layer_no], 'dp', axis=0, tiled=True)  93.5 us
    all_gather x1, waiting for transfers between devices, body(): lax.all_gather(w_down[layer_no], 'dp', axis=1, tiled=True)  89.2 us
    all_gather x1, waiting for transfers between devices, body(): lax.all_gather(w_gate[layer_no], 'dp', axis=0, tiled=True)  84.3 us
  transfers between devices with their start and end apart: 15, of which 13 were waited for; matrix products, arithmetic and copies ran while one was open for 6% of the time, Pallas kernels for 0%

commit v1 on v0

--- a/solution.py
+++ b/solution.py
@@ -1,6 +1,8 @@
 import jax
 import jax.numpy as jnp
 from jax import lax
+from jax.experimental import pallas as pl
+from jax.experimental.pallas import tpu as pltpu
 from jax.sharding import PartitionSpec as P
 
 HD = 64
@@ -303,9 +305,982 @@
     )
 
 
+ZN = 4
+MESH = pl.DeviceIdType.MESH
+BF = jnp.bfloat16
+F32 = jnp.float32
+LANE = 128
+
+
+def place():
+    dp = lax.axis_index("dp")
+    return dp // 4, (dp // 2) % 2, dp % 2, lax.axis_index("tensor")
+
+
+def dev(z, x, c, y):
+    return (z * 4 + x * 2 + c, y)
+
+
+def rid(z, x, c):
+    return (z * 2 + x) * 2 + c
+
+
+def lanes(r, width=LANE):
+    return pl.ds(pl.multiple_of(r * width, LANE), width)
+
+
+def rows(r, height):
+    return pl.ds(pl.multiple_of(r * height, 16), height)
+
+
+def greet(peers):
+    barrier = pltpu.get_barrier_semaphore()
+    for peer in peers:
+        pl.semaphore_signal(barrier, inc=1, device_id=peer, device_id_type=MESH)
+    pl.semaphore_wait(barrier, len(peers))
+
+
+class Wire:
+    def __init__(self, send_sem, recv_sem):
+        self.send_sem = send_sem
+        self.recv_sem = recv_sem
+        self.started = []
+
+    def make(self, src, dst, si, ri, to):
+        return pltpu.make_async_remote_copy(
+            src_ref=src,
+            dst_ref=dst,
+            send_sem=self.send_sem.at[si],
+            recv_sem=self.recv_sem.at[ri],
+            device_id=to,
+            device_id_type=MESH,
+        )
+
+    def send(self, src, dst, si, ri, to, cond=None):
+        def go():
+            self.make(src, dst, si, ri, to).start()
+
+        def done():
+            self.make(src, dst, si, ri, to).wait_send()
+
+        if cond is None:
+            go()
+            self.started.append(done)
+        else:
+            pl.when(cond)(go)
+            self.started.append(lambda: pl.when(cond)(done))
+
+    def arrived(self, dst, ri, to, cond=None):
+        def wait():
+            self.make(dst, dst, 0, ri, to).wait_recv()
+
+        if cond is None:
+            wait()
+        else:
+            pl.when(cond)(wait)
+
+    def drain(self):
+        for done in self.started:
+            done()
+
+
+def all_peers(z, x, c, y):
+    near = [dev(z, x, 1 - c, y), dev(z, 1 - x, c, y), dev(z, x, c, 1 - y)]
+    return near + [dev((z + d) % ZN, x, c, y) for d in (1, 2, 3)]
+
+
+def params(cid):
+    return pltpu.CompilerParams(
+        collective_id=cid, has_side_effects=True, vmem_limit_bytes=60 * 1024 * 1024
+    )
+
+
+def any_spec():
+    return pl.BlockSpec(memory_space=pl.ANY)
+
+
+def vm_spec():
+    return pl.BlockSpec(memory_space=pltpu.VMEM)
+
+
+def sems(n):
+    return pltpu.SemaphoreType.DMA((n,))
+
+
+def dot_nn(a, b):
+    return lax.dot_general(a, b, (((1,), (0,)), ((), ())), preferred_element_type=F32)
+
+
+def dot_nt(a, b):
+    return lax.dot_general(a, b, (((1,), (1,)), ((), ())), preferred_element_type=F32)
+
+
+def dot_tn(a, b):
+    return lax.dot_general(a, b, (((0,), (0,)), ((), ())), preferred_element_type=F32)
+
+
+def by_rows(height, step, one):
+    def wrapped(i, carry):
+        one(pl.ds(pl.multiple_of(i * step, step), step))
+        return carry
+
+    lax.fori_loop(0, height // step, wrapped, 0)
+
+
+def swap_halves(v):
+    lane = lax.broadcasted_iota(jnp.int32, v.shape, 1)
+    first = (lane % HD) < (HD // 2)
+    return jnp.where(first, pltpu.roll(v, LANE - HD // 2, 1), pltpu.roll(v, HD // 2, 1))
+
+
+def spread_pair(dst, pair):
+    lane = lax.broadcasted_iota(jnp.int32, pair.shape, 1)
+    low = lane < HD
+    turned = pltpu.roll(pair, HD, 1)
+    zero = jnp.zeros_like(pair)
+    dst[0] = jnp.where(low, pair, zero).astype(BF)
+    dst[1] = jnp.where(low, zero, turned).astype(BF)
+    dst[2] = jnp.where(low, turned, zero).astype(BF)
+    dst[3] = jnp.where(low, zero, pair).astype(BF)
+
+
+class Line:
+    def __init__(self, wire, own, buf, send_base, recv_base):
+        self.wire, self.own, self.buf = wire, own, buf
+        self.s, self.r = send_base, recv_base
+        z, x, c, y = place()
+        self.z, self.y = z, y
+        self.up, self.down = dev(z + 1, x, c, y), dev(z - 1, x, c, y)
+        self.other = dev(z, x, c, 1 - y)
+        self.seq, self.half = own.shape[0], own.shape[1] // 2
+
+    def blk(self, o, h):
+        return self.buf.at[rows(o, self.seq), lanes(h, self.half)]
+
+    def start(self):
+        z, wire = self.z, self.wire
+        src = self.own.at[:, lanes(self.y, self.half)]
+        dst = self.blk(z, self.y)
+        wire.send(src, dst, self.s + z, self.r + z, self.up, z < ZN - 1)
+        wire.send(src, dst, self.s + 4 + z, self.r + z, self.down, z > 0)
+
+    def relay(self, s):
+        z, wire = self.z, self.wire
+        for o, cond, fwd, to, frm, base in (
+            (z - s, z >= s, z < ZN - 1, self.up, self.down, 0),
+            (z + s, z + s < ZN, z > 0, self.down, self.up, 4),
+        ):
+            b = self.blk(o, self.y)
+            wire.arrived(b, self.r + o, frm, cond)
+            wire.send(b, b, self.s + base + o, self.r + o, to, cond & fwd)
+            wire.send(b, b, self.s + 8 + o, self.r + 4 + o, self.other, cond)
+
+    def finish(self):
+        for o in range(ZN):
+            self.wire.arrived(self.blk(o, 1 - self.y), self.r + 4 + o, self.other, self.z != o)
+
+
+class Tree:
+    def __init__(self, wire, own, blk, send_base, recv_base):
+        self.wire, self.own, self.blk = wire, own, blk
+        self.s, self.r = send_base, recv_base
+        self.z, self.x, self.c, y = place()
+        z, x, c = self.z, self.x, self.c
+        self.up, self.down = dev(z + 1, x, c, y), dev(z - 1, x, c, y)
+        self.side, self.twin = dev(z, 1 - x, c, y), dev(z, x, 1 - c, y)
+
+    def start(self):
+        z, wire = self.z, self.wire
+        d = self.blk(rid(z, self.x, self.c))
+        wire.send(self.own, d, self.s + z, self.r + z, self.up, z < ZN - 1)
+        wire.send(self.own, d, self.s + 4 + z, self.r + z, self.down, z > 0)
+        wire.send(self.own, d, self.s + 8 + z, self.r + 4 + z, self.side)
+        k = z * 2 + self.x
+        wire.send(self.own, d, self.s + 12 + k, self.r + 8 + k, self.twin)
+
+    def relay(self, s):
+        z, wire = self.z, self.wire
+        for o, cond, fwd, to, frm, base in (
+            (z - s, z >= s, z < ZN - 1, self.up, self.down, 0),
+            (z + s, z + s < ZN, z > 0, self.down, self.up, 4),
+        ):
+            b = self.blk(rid(o, self.x, self.c))
+            wire.arrived(b, self.r + o, frm, cond)
+            wire.send(b, b, self.s + base + o, self.r + o, to, cond & fwd)
+            wire.send(b, b, self.s + 8 + o, self.r + 4 + o, self.side, cond)
+            k = o * 2 + self.x
+            wire.send(b, b, self.s + 12 + k, self.r + 8 + k, self.twin, cond)
+
+    def across(self, s):
+        z = self.z
+        todo = ((z, None),) if s == 0 else ((z - s, z >= s), (z + s, z + s < ZN))
+        for o, cond in todo:
+            b = self.blk(rid(o, 1 - self.x, self.c))
+            self.wire.arrived(b, self.r + 4 + o, self.side, cond)
+            k = o * 2 + 1 - self.x
+            self.wire.send(b, b, self.s + 12 + k, self.r + 8 + k, self.twin, cond)
+
+    def finish(self):
+        for o in range(ZN):
+            for xx in (0, 1):
+                b = self.blk(rid(o, xx, 1 - self.c))
+                self.wire.arrived(b, self.r + 8 + o * 2 + xx, self.twin)
+
+
+def front_kernel(
+    resid, wq_l, wk_l, wv_l, wo_l, ga_l, wg_l, wu_l, wd_l, cot, cos_t, sin_t, mask,
+    wqkv, wo, ga, w3, dres, n1, q, kv, ctx, mid, normed,
+    qkv_l, w3_l, dres_l, kx, vx, attn, part, nrm, ss, rs, ls,
+):
+    z, x, c, y = place()
+    units = w3.shape[1]
+    seq, width = resid.shape
+    q_width = q.shape[1]
+    pairs = q_width // LANE
+    wire = Wire(ss, rs)
+    side, twin, other = dev(z, 1 - x, c, y), dev(z, x, 1 - c, y), dev(z, x, c, 1 - y)
+    qkv_l[:, pl.ds(0, q_width)] = wq_l[0]
+    qkv_l[:, pl.ds(q_width, LANE)] = wk_l[0]
+    qkv_l[:, pl.ds(q_width + LANE, LANE)] = wv_l[0]
+    greet(all_peers(z, x, c, y))
+
+    def qkv_blk(r):
+        return wqkv.at[pl.ds(pl.multiple_of(r * LANE, LANE), LANE), :]
+
+    def wo_blk(r):
+        return wo.at[:, lanes(r)]
+
+    def ga_blk(r):
+        return ga.at[:, lanes(r)]
+
+    def ffn(r):
+        return w3.at[:, :, lanes(r)]
+
+    t_qkv = Tree(wire, qkv_l, qkv_blk, 0, 0)
+    t_wo = Tree(wire, wo_l.at[0], wo_blk, 20, 16)
+    t_ga = Tree(wire, ga_l, ga_blk, 40, 32)
+    l_dres = Line(wire, dres_l, dres, 76, 64)
+    l_norm = Line(wire, nrm, normed, 88, 72)
+    mine = rid(z, x, c)
+    t_ga.start()
+    t_qkv.start()
+    own = [
+        pltpu.make_async_copy(qkv_l, qkv_blk(mine), ls.at[0]),
+        pltpu.make_async_copy(wo_l.at[0], wo_blk(mine), ls.at[1]),
+        pltpu.make_async_copy(ga_l, ga_blk(mine), ls.at[2]),
+    ]
+    for cp in own:
+        cp.start()
+
+    def round_cot(r):
+        dres_l[r, :] = cot[r, :].astype(BF)
+
+    by_rows(seq, 16, round_cot)
+    for s in (1, 2, 3):
+        t_ga.relay(s)
+    for s in (0, 1, 2, 3):
+        t_ga.across(s)
+    t_qkv.relay(1)
+    t_qkv.across(0)
+    t_ga.finish()
+    own[2].wait()
+    gain_one = ga[pl.ds(0, 8), :].astype(F32)[0:1]
+    gain_two = ga[pl.ds(0, 8), :].astype(F32)[1:2]
+
+    def norm_one(r):
+        v = resid[r, :]
+        recip = lax.rsqrt(jnp.mean(v * v, axis=-1, keepdims=True) + epsilon)
+        n1[r, :] = (v * recip * gain_one).astype(BF)
+
+    by_rows(seq, 16, norm_one)
+    t_qkv.relay(2)
+    t_qkv.across(1)
+    t_qkv.relay(3)
+    t_wo.start()
+
+    def turn(i, carry):
+        cut = lanes(i)
+        w3_l[0, pl.ds(pl.multiple_of(i * LANE, LANE), LANE), :] = (
+            wg_l[0, :, cut].astype(F32).T.astype(BF)
+        )
+        w3_l[1, pl.ds(pl.multiple_of(i * LANE, LANE), LANE), :] = (
+            wu_l[0, :, cut].astype(F32).T.astype(BF)
+        )
+        return carry
+
+    lax.fori_loop(0, w3_l.shape[1] // LANE, turn, 0)
+    by_rows(w3_l.shape[1], 64, lambda r: w3_l.at[2].__setitem__((r, slice(None)), wd_l[0, r, :]))
+    t_qkv.across(2)
+    t_qkv.across(3)
+    t_wo.relay(1)
+    t_qkv.finish()
+    own[0].wait()
+
+    def turned(v):
+        return v * cos_t[...] + swap_halves(v) * sin_t[...]
+
+    def q_tile(j, carry):
+        acc = dot_nn(n1[...], wqkv[:, lanes(j, 2 * LANE)])
+        for h in (0, 1):
+            q[:, lanes(2 * j + h)] = turned(acc[:, h * LANE : (h + 1) * LANE]).astype(BF)
+        return carry
+
+    lax.fori_loop(0, pairs // 2, q_tile, 0)
+    acc = dot_nn(n1[...], wqkv[:, pl.ds(q_width, 2 * LANE)])
+    key = turned(acc[:, :LANE]).astype(BF)
+    val = acc[:, LANE:].astype(BF)
+    kv[:, pl.ds(0, LANE)] = key
+    kv[:, pl.ds(LANE, LANE)] = val
+    spread_pair(kx, key.astype(F32))
+    spread_pair(vx, val.astype(F32))
+    t_wo.relay(2)
+    t_wo.across(0)
+
+    def pair(p, carry):
+        qp = q[:, lanes(p)]
+        g = p // (pairs // 2)
+        out = jnp.zeros((seq, LANE), F32)
+        for h in (0, 1):
+            s = dot_nt(qp, kx[2 * g + h]) * HD ** (-0.5)
+            s = jnp.where(mask[...] > 0.0, s, masked_score)
+            top = jnp.max(s, axis=-1, keepdims=True)
+            lse = top + jnp.log(jnp.sum(jnp.exp(s - top), axis=-1, keepdims=True))
+            out = out + dot_nn(jnp.exp(s - lse).astype(BF), vx[2 * g + h])
+        ctx[:, lanes(p)] = out.astype(BF)
+        return carry
+
+    lax.fori_loop(0, pairs // 2, pair, 0)
+    t_wo.relay(3)
+    for d in (2, 1, 3):
+        zt = (z + d) % ZN
+        wire.send(w3_l.at[:, rows(zt, units), :], ffn(mine), 60 + d - 1, 48 + z, dev(zt, x, c, y))
+    mine3 = w3_l.at[:, rows(z, units), :]
+    wire.send(mine3, ffn(mine), 64 + z, 52 + z, side)
+    wire.send(mine3, ffn(mine), 68 + z * 2 + x, 56 + z * 2 + x, twin)
+    l_dres.start()
+    own += [
+        pltpu.make_async_copy(mine3, ffn(mine), ls.at[3]),
+        pltpu.make_async_copy(dres_l, dres.at[rows(z, seq), :], ls.at[4]),
+    ]
+    own[3].start()
+    own[4].start()
+    lax.fori_loop(pairs // 2, pairs, pair, 0)
+    for s in (1, 2, 3):
+        t_wo.across(s)
+    t_wo.finish()
+    own[1].wait()
+
+    def out_tile(j, carry):
+        cut = lanes(j, 2 * LANE)
+        attn[:, cut] = dot_nn(ctx[...], wo[:, cut]).astype(BF)
+        return carry
+
+    lax.fori_loop(0, width // (2 * LANE), out_tile, 0)
+    wire.send(attn, part, 100, 80, other)
+    l_dres.relay(1)
+
+    def ffn_in(d):
+        o = (z + ZN - d) % ZN
+        b = ffn(rid(o, x, c))
+        wire.arrived(b, 48 + o, dev(o, x, c, y))
+        wire.send(b, b, 64 + o, 52 + o, side)
+        wire.send(b, b, 68 + o * 2 + x, 56 + o * 2 + x, twin)
+
+    def ffn_across(d):
+        o = (z + ZN - d) % ZN
+        b = ffn(rid(o, 1 - x, c))
+        wire.arrived(b, 52 + o, side)
+        k = o * 2 + 1 - x
+        wire.send(b, b, 68 + k, 56 + k, twin)
+
+    ffn_in(2)
+    wire.arrived(part, 80, other)
+
+    def second(r):
+        m = resid[r, :] + (attn[r, :].astype(F32) + part[r, :].astype(F32))
+        mid[r, :] = m
+        recip = lax.rsqrt(jnp.mean(m * m, axis=-1, keepdims=True) + epsilon)
+        nrm[r, :] = (m * recip * gain_two).astype(BF)
+
+    by_rows(seq, 16, second)
+    l_norm.start()
+    own.append(pltpu.make_async_copy(nrm, normed.at[rows(z, seq), :], ls.at[5]))
+    own[5].start()
+    ffn_in(1)
+    l_dres.relay(2)
+    l_norm.relay(1)
+    ffn_across(0)
+    ffn_in(3)
+    l_dres.relay(3)
+    l_norm.relay(2)
+    l_norm.relay(3)
+    for d in (2, 1, 3):
+        ffn_across(d)
+    for o in range(ZN):
+        for xx in (0, 1):
+            wire.arrived(ffn(rid(o, xx, 1 - c)), 56 + o * 2 + xx, twin)
+    l_dres.finish()
+    l_norm.finish()
+    wire.drain()
+    for cp in own[3:]:
+        cp.wait()
+
+
+def front(resid, w_query, w_key, w_value, w_out, gains, w_gate, w_up, w_down, cot, cos_t, sin_t, mask):
+    seq, width = resid.shape
+    q_width, out_rows = w_query.shape[2], w_out.shape[1]
+    total = q_width + 2 * LANE
+    units = w_gate.shape[2] // ZN
+    pair_shape = (4, seq, LANE)
+    return pl.pallas_call(
+        front_kernel,
+        name="front",
+        out_shape=(
+            jax.ShapeDtypeStruct((width, total), BF),
+            jax.ShapeDtypeStruct((out_rows, width), BF),
+            jax.ShapeDtypeStruct((16, width), BF),
+            jax.ShapeDtypeStruct((3, units, width), BF),
+            jax.ShapeDtypeStruct((seq * ZN, width), BF),
+            jax.ShapeDtypeStruct((seq, width), BF),
+            jax.ShapeDtypeStruct((seq, q_width), BF),
+            jax.ShapeDtypeStruct((seq, 2 * LANE), BF),
+            jax.ShapeDtypeStruct((seq, q_width), BF),
+            jax.ShapeDtypeStruct((seq, width), F32),
+            jax.ShapeDtypeStruct((seq * ZN, width), BF),
+        ),
+        in_specs=[vm_spec()] * 13,
+        out_specs=[vm_spec()] * 3 + [any_spec()] * 2 + [vm_spec()] * 5 + [any_spec()],
+        scratch_shapes=[
+            pltpu.VMEM((LANE, total), BF),
+            pltpu.VMEM((3, units * ZN, LANE), BF),
+            pltpu.VMEM((seq, width), BF),
+            pltpu.VMEM(pair_shape, BF),
+            pltpu.VMEM(pair_shape, BF),
+            pltpu.VMEM((seq, width), BF),
+            pltpu.VMEM((seq, width), BF),
+            pltpu.VMEM((seq, width), BF),
+            sems(101),
+            sems(81),
+            sems(6),
+        ],
+        compiler_params=params(0),
+    )(resid, w_query, w_key, w_value, w_out, gains, w_gate, w_up, w_down, cot, cos_t, sin_t, mask)
+
+
+def add_into(dst, src, height, step):
+    def one(r):
+        dst[r, :] = (dst[r, :].astype(F32) + src[r, :].astype(F32)).astype(dst.dtype)
+
+    by_rows(height, step, one)
+
+
+class Chain:
+    def __init__(self, wire, held, zin, height, step, send_base, recv_base):
+        self.wire, self.held, self.zin = wire, held, zin
+        self.height, self.step = height, step
+        self.s, self.r = send_base, recv_base
+        self.z, x, c, y = place()
+        self.up, self.down = dev(self.z + 1, x, c, y), dev(self.z - 1, x, c, y)
+
+    def inbound(self, o, slot, frm, cond):
+        self.wire.arrived(self.zin(slot), self.r + slot, frm, cond)
+
+        @pl.when(cond)
+        def _():
+            add_into(self.held(o), self.zin(slot), self.height, self.step)
+
+    def outward(self, t, ready):
+        z = self.z
+        for o, cond, more, to, frm, base, slot in (
+            (z + t, z + t < ZN, z > 0, self.up, self.down, 0, z + t),
+            (z - t, z >= t, z < ZN - 1, self.down, self.up, 4, 4 if t == 1 else z - t),
+        ):
+            ready(o, cond)
+            self.inbound(o, o, frm, cond & more)
+            self.wire.send(
+                self.held(o), self.zin(slot), self.s + base + o, self.r + slot, to, cond
+            )
+
+    def home(self):
+        z = self.z
+        self.inbound(z, z, self.down, z > 0)
+        self.inbound(z, 4, self.up, z < ZN - 1)
+
+
+class Fold:
+    def __init__(self, wire, part, cin, xin, zin, height, step, send_base, recv_base):
+        self.wire, self.part, self.cin, self.xin = wire, part, cin, xin
+        self.height, self.step = height, step
+        self.s, self.r = send_base, recv_base
+        self.z, self.x, self.c, y = place()
+        z, x, c = self.z, self.x, self.c
+        self.side, self.twin = dev(z, 1 - x, c, y), dev(z, x, 1 - c, y)
+        self.chain = Chain(
+            wire, lambda o: xin.at[o], lambda s: zin.at[s], height, step, self.s + 12, self.r + 12
+        )
+
+    def order(self):
+        return [(self.z + d) % ZN for d in (2, 1, 3, 0)]
+
+    def to_twin(self):
+        for xx in (1 - self.x, self.x):
+            for o in self.order():
+                k = o * 2 + xx
+                self.wire.send(
+                    self.part(k * 2 + 1 - self.c), self.cin.at[k], self.s + k, self.r + k, self.twin
+                )
+
+    def from_twin(self, k):
+        self.wire.arrived(self.cin.at[k], self.r + k, self.twin)
+        add_into(self.cin.at[k], self.part(k * 2 + self.c), self.height, self.step)
+
+    def across(self):
+        for o in self.order():
+            k = o * 2 + 1 - self.x
+            self.from_twin(k)
+            self.wire.send(self.cin.at[k], self.xin.at[o], self.s + 8 + o, self.r + 8 + o, self.side)
+
+    def stay(self):
+        for o in self.order():
+            self.from_twin(o * 2 + self.x)
+
+    def ready(self, o, cond):
+        self.wire.arrived(self.xin.at[o], self.r + 8 + o, self.side, cond)
+
+        @pl.when(cond)
+        def _():
+            add_into(self.xin.at[o], self.cin.at[o * 2 + self.x], self.height, self.step)
+
+    def outward(self, t):
+        self.chain.outward(t, self.ready)
+
+    def home(self):
+        self.ready(self.z, self.z >= 0)
+        self.chain.home()
+        return self.xin.at[self.z]
+
+
+def back_kernel(
+    dn_p, feed_p, g3_p, mid, cot, resid, ga, n1, q, kv, ctx, wqkv, wo, cos_t, sin_t, mask,
+    hidden, grad_in, g3, gq_out, gk_out, gv_out, go_out, gains_out,
+    fown, yin, zin, gbuf, cin, xin, gq_p, go_p, gp, qc, qx, qz, oc, ox, oz, gc, gx, gz,
+    dn, feed, mid_b, dctx, dqkv, dn1, dn1_o, kx, vx, kacc, vacc, wbuf, gs, gr, ss, rs, ls,
+):
+    z, x, c, y = place()
+    units = g3_p.shape[1]
+    seq, width = mid.shape
+    half = width // 2
+    q_width = q.shape[1]
+    pairs = q_width // LANE
+    out_rows = wo.shape[0]
+    wire = Wire(ss, rs)
+    side, twin, other = dev(z, 1 - x, c, y), dev(z, x, 1 - c, y), dev(z, x, c, 1 - y)
+    ring = [(z + d) % ZN for d in (2, 1, 3, 0)]
+    greet(all_peers(z, x, c, y))
+
+    def y_out(src, k):
+        for t in (3, 2, 1):
+            for o, cond in ((z + t, z + t < ZN), (z - t, z >= t)):
+                s = src.at[rows(o, seq), lanes(1 - y, half)]
+                wire.send(s, yin.at[k, o], k * 4 + o, k * 4 + o, other, cond)
+        s = src.at[rows(z, seq), lanes(1 - y, half)]
+        wire.send(s, yin.at[k, z], k * 4 + z, k * 4 + z, other)
+
+    y_out(dn_p, 0)
+    for k in range(8):
+        wire.send(g3_p.at[:, :, lanes(k * 2 + 1 - c)], cin.at[k], 26 + k, 20 + k, twin)
+    ks = [o * 2 + 1 - x for o in ring] + [o * 2 + x for o in ring]
+
+    def load(i):
+        return pltpu.make_async_copy(
+            g3_p.at[:, :, lanes(ks[i] * 2 + c)], gbuf.at[i % 2], ls.at[i % 2]
+        )
+
+    def own_half(o):
+        return pltpu.make_async_copy(
+            feed_p.at[rows(o, seq), lanes(y, half)], fown.at[o], ls.at[2 + o]
+        )
+
+    def add3(dst, src):
+        for m in range(3):
+            add_into(dst.at[m], src.at[m], units, 64)
+
+    load(0).start()
+    for i in range(8):
+        if i < 7:
+            load(i + 1).start()
+        load(i).wait()
+        wire.arrived(cin.at[ks[i]], 20 + ks[i], twin)
+        add3(cin.at[ks[i]], gbuf.at[i % 2])
+        if i < 4:
+            o = ring[i]
+            wire.send(cin.at[ks[i]], xin.at[o], 34 + o, 28 + o, side)
+    for o in range(ZN):
+        own_half(o).start()
+
+    def chain_of(k):
+        return Chain(
+            wire, lambda o: yin.at[k, o], lambda s: zin.at[k, s], seq, 16, 8 + k * 8, 8 + k * 5
+        )
+
+    def dn_ready(o, cond):
+        wire.arrived(yin.at[0, o], o, other, cond)
+
+        @pl.when(cond)
+        def _():
+            def one(r):
+                mine = dn_p[pl.ds(pl.multiple_of(o * seq, 16) + r.start, 16), lanes(y, half)]
+                yin[0, o, r, :] = (yin[0, o, r, :].astype(F32) + mine.astype(F32)).astype(BF)
+
+            by_rows(seq, 16, one)
+
+    line = chain_of(0)
+    for t in (3, 2, 1):
+        line.outward(t, dn_ready)
+    dn_ready(z, z >= 0)
+    line.home()
+    blk = dn.at[:, lanes(y, half)]
+
+    def keep_dn(r):
+        dn[r, lanes(y, half)] = yin[0, z, r, :]
+
+    by_rows(seq, 16, keep_dn)
+    wire.send(blk, blk, 24, 18, other)
+    y_out(feed_p, 1)
+
+    def ffn_z(i):
+        o = ring[i]
+        wire.arrived(xin.at[o], 28 + o, side)
+        add3(xin.at[o], cin.at[o * 2 + x])
+        d = (2, 1, 3, 0)[i]
+        if d:
+            wire.send(xin.at[o], g3.at[:, rows(z, units), :], 38 + d - 1, 32 + z, dev(o, x, c, y))
+        else:
+            pltpu.make_async_copy(xin.at[o], g3.at[:, rows(z, units), :], ls.at[6]).start()
+
+    ffn_z(0)
+    ffn_z(1)
+    spread_pair(kx, kv[:, pl.ds(0, LANE)].astype(F32))
+    spread_pair(vx, kv[:, pl.ds(LANE, LANE)].astype(F32))
+    kacc[...] = jnp.zeros_like(kacc)
+    vacc[...] = jnp.zeros_like(vacc)
+    gp[...] = jnp.zeros_like(gp)
+    gain_one = ga[pl.ds(0, 8), :].astype(F32)[0:1]
+    gain_two = ga[pl.ds(0, 8), :].astype(F32)[1:2]
+    wire.arrived(dn.at[:, lanes(1 - y, half)], 18, other)
+
+    def norm_two(r):
+        v, g = mid[r, :], dn[r, :].astype(F32)
+        recip = lax.rsqrt(jnp.mean(v * v, axis=-1, keepdims=True) + epsilon)
+        e = g * gain_two
+        d = recip * e - v * (recip * recip * recip) * jnp.mean(e * v, axis=-1, keepdims=True)
+        out = cot[r, :] + d
+        grad_in[r, :] = out
+        mid_b[r, :] = out.astype(BF)
+        t = g * v * recip
+        gp[pl.ds(8, 8), :] += t[:8] + t[8:]
+
+    by_rows(seq, 16, norm_two)
+
+    def out_grad(i, carry):
+        cut = lanes(i, 2 * LANE)
+        for h in range(2):
+            hh = pl.ds(h * (out_rows // 2), out_rows // 2)
+            go_p[hh, cut] = dot_tn(ctx[:, hh], mid_b[:, cut]).astype(BF)
+        return carry
+
+    lax.fori_loop(0, width // (2 * LANE), out_grad, 0)
+    f_o = Fold(wire, lambda r: go_p.at[:, lanes(r)], oc, ox, oz, out_rows, 64, 61, 53)
+    f_q = Fold(
+        wire,
+        lambda r: gq_p.at[pl.ds(pl.multiple_of(r * LANE, LANE), LANE), :],
+        qc, qx, qz, LANE, 16, 41, 36,
+    )
+    f_g = Fold(wire, lambda r: gp.at[:, lanes(r)], gc, gx, gz, 16, 16, 81, 70)
+    f_o.to_twin()
+
+    def ctx_grad(j, carry):
+        cut = lanes(j, 2 * LANE)
+        dctx[:, cut] = dot_nt(mid_b[...], wo[cut, :]).astype(BF)
+        return carry
+
+    lax.fori_loop(0, q_width // (2 * LANE), ctx_grad, 0)
+    ffn_z(2)
+    ffn_z(3)
+    f_o.across()
+
+    def back_turned(v):
+        return v * cos_t[...] - swap_halves(v) * sin_t[...]
+
+    def pair(p, carry):
+        qp, dc = q[:, lanes(p)], dctx[:, lanes(p)]
+        g = p // (pairs // 2)
+        prod = dc.astype(F32) * ctx[:, lanes(p)].astype(F32)
+        low = lax.broadcasted_iota(jnp.int32, prod.shape, 1) < HD
+        dq = jnp.zeros((seq, LANE), F32)
+        for h in (0, 1):
+            i = 2 * g + h
+            s = dot_nt(qp, kx[i]) * HD ** (-0.5)
+            s = jnp.where(mask[...] > 0.0, s, masked_score)
+            top = jnp.max(s, axis=-1, keepdims=True)
+            lse = top + jnp.log(jnp.sum(jnp.exp(s - top), axis=-1, keepdims=True))
+            full = jnp.exp(s - lse)
+            delta = jnp.sum(jnp.where(low if h == 0 else ~low, prod, 0.0), axis=-1, keepdims=True)
+            ds = (full * (dot_nt(dc, vx[i]) - delta)).astype(BF)
+            dq = dq + dot_nn(ds, kx[i])
+            kacc[i] += dot_tn(ds, qp)
+            vacc[i] += dot_tn(full.astype(BF), dc)
+        dqkv[:, lanes(p)] = back_turned(dq * HD ** (-0.5)).astype(BF)
+        return carry
+
+    lax.fori_loop(0, pairs, pair, 0)
+
+    def joined(acc):
+        low = lax.broadcasted_iota(jnp.int32, (seq, LANE), 1) < HD
+        return jnp.where(
+            low, acc[0] + pltpu.roll(acc[1], HD, 1), acc[3] + pltpu.roll(acc[2], HD, 1)
+        )
+
+    dqkv[:, pl.ds(q_width, LANE)] = back_turned(joined(kacc) * HD ** (-0.5)).astype(BF)
+    dqkv[:, pl.ds(q_width + LANE, LANE)] = joined(vacc).astype(BF)
+
+    def w_tile(j, slot):
+        r = pl.ds(pl.multiple_of(j * 2 * LANE, 2 * LANE), 2 * LANE)
+        return pltpu.make_async_copy(wqkv.at[r, :], wbuf.at[slot], ls.at[7 + slot])
+
+    w_tile(0, 0).start()
+
+    def in_grad(r, carry):
+        gq_p[pl.ds(pl.multiple_of(r * LANE, LANE), LANE), :] = dot_tn(
+            n1[:, lanes(r)], dqkv[...]
+        ).astype(BF)
+        return carry
+
+    lax.fori_loop(0, width // LANE, in_grad, 0)
+    f_q.to_twin()
+    tiles = width // (2 * LANE)
+    for j in range(tiles):
+        if j + 1 < tiles:
+            w_tile(j + 1, (j + 1) % 2).start()
+        w_tile(j, j % 2).wait()
+        dn1[:, pl.ds(j * 2 * LANE, 2 * LANE)] = dot_nt(dqkv[...], wbuf[j % 2]).astype(BF)
+    wire.send(dn1, dn1_o, 101, 87, other)
+    f_q.across()
+
+    def gain_part(r):
+        v = resid[r, :]
+        recip = lax.rsqrt(jnp.mean(v * v, axis=-1, keepdims=True) + epsilon)
+        t = dn1[r, :].astype(F32) * v * recip
+        gp[pl.ds(0, 8), :] += t[:8] + t[8:]
+
+    by_rows(seq, 16, gain_part)
+    f_g.to_twin()
+    f_g.across()
+    f_o.stay()
+    for t in (3, 2, 1):
+        f_o.outward(t)
+
+    for o in range(ZN):
+        own_half(o).wait()
+
+    def feed_ready(o, cond):
+        wire.arrived(yin.at[1, o], 4 + o, other, cond)
+
+        @pl.when(cond)
+        def _():
+            add_into(yin.at[1, o], fown.at[o], seq, 16)
+
+    line = chain_of(1)
+    for t in (3, 2, 1):
+        line.outward(t, feed_ready)
+    f_q.stay()
+    f_g.stay()
+    for t in (3, 2, 1):
+        f_q.outward(t)
+        f_g.outward(t)
+    feed_ready(z, z >= 0)
+    line.home()
+    fb = feed.at[:, lanes(y, half)]
+
+    def keep_feed(r):
+        feed[r, lanes(y, half)] = yin[1, z, r, :]
+
+    by_rows(seq, 16, keep_feed)
+    wire.send(fb, fb, 25, 19, other)
+    wire.arrived(dn1_o, 87, other)
+
+    def norm_one(r):
+        v = resid[r, :]
+        g = dn1[r, :].astype(F32) + dn1_o[r, :].astype(F32)
+        recip = lax.rsqrt(jnp.mean(v * v, axis=-1, keepdims=True) + epsilon)
+        e = g * gain_one
+        d = recip * e - v * (recip * recip * recip) * jnp.mean(e * v, axis=-1, keepdims=True)
+        grad_in[r, :] += d
+
+    by_rows(seq, 16, norm_one)
+    done = f_o.home()
+    by_rows(out_rows, 64, lambda r: go_out.at[0].__setitem__((r, slice(None)), done[r, :].astype(F32)))
+    mine = f_g.home()
+    gs[...] = mine[...]
+    wire.send(gs, gr, 102, 88, other)
+    got = f_q.home()
+    cut_k, cut_v = pl.ds(q_width, LANE), pl.ds(q_width + LANE, LANE)
+    gq_out[0] = got[:, pl.ds(0, q_width)].astype(F32)
+    gk_out[0] = got[:, cut_k].astype(F32)
+    gv_out[0] = got[:, cut_v].astype(F32)
+    wire.arrived(feed.at[:, lanes(1 - y, half)], 19, other)
+
+    def last(r):
+        hidden[r, :] = mid[r, :] + feed[r, :].astype(F32)
+
+    by_rows(seq, 16, last)
+    wire.arrived(gr, 88, other)
+    first = jnp.sum(gs[pl.ds(0, 8), :] + gr[pl.ds(0, 8), :], axis=0, keepdims=True)
+    second = jnp.sum(gs[pl.ds(8, 8), :], axis=0, keepdims=True)
+    row = lax.broadcasted_iota(jnp.int32, (8, LANE), 0)
+    gains_out[...] = jnp.where(row == 0, first, second)
+    for d in (1, 2, 3):
+        o = (z + ZN - d) % ZN
+        wire.arrived(g3.at[:, rows(o, units), :], 32 + o, dev(o, x, c, y))
+    wire.drain()
+    pltpu.make_async_copy(xin.at[z], g3.at[:, rows(z, units), :], ls.at[6]).wait()
+
+
+def back(dn_p, feed_p, g3_p, mid, cot, resid, ga, n1, q, kv, ctx, wqkv, wo, cos_t, sin_t, mask):
+    seq, width = mid.shape
+    units = g3_p.shape[1]
+    q_width, total = q.shape[1], wqkv.shape[1]
+    out_rows = wo.shape[0]
+    half = width // 2
+
+    def vm(*shape, dtype=BF):
+        return pltpu.VMEM(shape, dtype)
+
+    return pl.pallas_call(
+        back_kernel,
+        name="back",
+        out_shape=(
+            jax.ShapeDtypeStruct((seq, width), F32),
+            jax.ShapeDtypeStruct((seq, width), F32),
+            jax.ShapeDtypeStruct((3, units * ZN, LANE), BF),
+            jax.ShapeDtypeStruct((1, LANE, q_width), F32),
+            jax.ShapeDtypeStruct((1, LANE, LANE), F32),
+            jax.ShapeDtypeStruct((1, LANE, LANE), F32),
+            jax.ShapeDtypeStruct((1, out_rows, LANE), F32),
+            jax.ShapeDtypeStruct((8, LANE), F32),
+        ),
+        in_specs=[vm_spec()] + [any_spec()] * 2 + [vm_spec()] * 8 + [any_spec()] + [vm_spec()] * 4,
+        out_specs=[vm_spec()] * 2 + [any_spec()] + [vm_spec()] * 5,
+        scratch_shapes=[
+            vm(ZN, seq, half),
+            vm(2, ZN, seq, half),
+            vm(2, 5, seq, half),
+            vm(2, 3, units, LANE),
+            vm(8, 3, units, LANE),
+            vm(4, 3, units, LANE),
+            vm(width, total),
+            vm(out_rows, width),
+            vm(16, width, dtype=F32),
+            vm(8, LANE, total),
+            vm(4, LANE, total),
+            vm(5, LANE, total),
+            vm(8, out_rows, LANE),
+            vm(4, out_rows, LANE),
+            vm(5, out_rows, LANE),
+            vm(8, 16, LANE, dtype=F32),
+            vm(4, 16, LANE, dtype=F32),
+            vm(5, 16, LANE, dtype=F32),
+            vm(seq, width),
+            vm(seq, width),
+            vm(seq, width),
+            vm(seq, q_width),
+            vm(seq, total),
+            vm(seq, width),
+            vm(seq, width),
+            vm(4, seq, LANE),
+            vm(4, seq, LANE),
+            vm(4, seq, LANE, dtype=F32),
+            vm(4, seq, LANE, dtype=F32),
+            vm(2, 2 * LANE, total),
+            vm(16, LANE, dtype=F32),
+            vm(16, LANE, dtype=F32),
+            sems(103),
+            sems(89),
+            sems(9),
+        ],
+        compiler_params=pltpu.CompilerParams(
+            collective_id=1, has_side_effects=True, vmem_limit_bytes=67043328
+        ),
+    )(dn_p, feed_p, g3_p, mid, cot, resid, ga, n1, q, kv, ctx, wqkv, wo, cos_t, sin_t, mask)
+
+
+def fast_body(
+    hidden_in,
+    segment_ids,
+    gain_attn,
+    w_query,
+    w_key,
+    w_value,
+    w_out,
+    gain_ffn,
+    w_gate,
+    w_up,
+    w_down,
+    cotangent,
+):
+    cos_t, sin_t = rope_tables(segment_positions(segment_ids))
+    cos_w = jnp.tile(cos_t[0], (1, 4))
+    sin_w = jnp.tile(jnp.concatenate([-sin_t[0], sin_t[0]], axis=1), (1, 2))
+    mask = attention_mask(segment_ids)[0, 0, 0].astype(F32)
+    gains = jnp.concatenate([gain_attn, gain_ffn, jnp.zeros((14, LANE), BF)], axis=0)
+    resid = hidden_in
+    wqkv, wo, ga, w3, dres_all, n1, q, kv, ctx, middle, normed_all = front(
+        resid, w_query, w_key, w_value, w_out, gains, w_gate, w_up, w_down, cotangent,
+        cos_w, sin_w, mask,
+    )
+    gate = contract_cols(normed_all, w3[0])
+    up_proj = contract_cols(normed_all, w3[1])
+    sigma = jax.nn.sigmoid(gate)
+    hidden_act = (gate * sigma * up_proj).astype(BF)
+    grad_hidden = contract_cols(dres_all, w3[2])
+    grad_gate_b = (grad_hidden * up_proj * sigma * (1.0 + gate * (1.0 - sigma))).astype(BF)
+    grad_up_b = (grad_hidden * (gate * sigma)).astype(BF)
+    feed_p = jnp.dot(hidden_act, w3[2], preferred_element_type=F32).astype(BF)
+    dn_p = (
+        jnp.dot(grad_gate_b, w3[0], preferred_element_type=F32)
+        + jnp.dot(grad_up_b, w3[1], preferred_element_type=F32)
+    ).astype(BF)
+    g3_p = jnp.stack(
+        [
+            contract_rows(grad_gate_b, normed_all).astype(BF),
+            contract_rows(grad_up_b, normed_all).astype(BF),
+            contract_rows(hidden_act, dres_all).astype(BF),
+        ]
+    )
+    hidden_out, grad_input, g3, gq, gk, gv, go, gains_g = back(
+        dn_p, feed_p, g3_p, middle, cotangent, resid, ga, n1, q, kv, ctx, wqkv, wo,
+        cos_w, sin_w, mask,
+    )
+    return (
+        hidden_out,
+        grad_input,
+        gains_g[0:1],
+        gq,
+        gk,
+        gv,
+        go,
+        gains_g[1:2],
+        g3[0].T.astype(F32)[None],
+        g3[1].T.astype(F32)[None],
+        g3[2].astype(F32)[None],
+    )
+
+
 def solution(mesh):
+    small = mesh.shape["dp"] == 16 and mesh.shape["tensor"] == 2
+    chosen = fast_body if small else body
     return jax.shard_map(
-        body,
+        chosen,
         mesh=mesh,
         in_specs=(
             P("dp", None),

time: 1680 us -> 380 us (0.23)
  waiting for transfers between devices: 1350 us -> 0 us
  Pallas kernels: 0 us -> 323 us
  blocking collectives: 145 us -> 0 us
  matrix products: 126 us -> 28.9 us
    reduce_scatter x7 -> x0, waiting for transfers between devices: 964 us -> none  [the longest x1 232 us: backward_layer(): lax.psum_scatter(grad_gate_w, 'dp', scatter_dimension=0, tiled=True)]
    pallas_call x0 -> x2, Pallas kernels: none -> 323 us  [the longest x1 162 us: back(): pl.pallas_call(back_kernel, name='back', out_shape=(jax.ShapeDtypeStruct(...]
    all_gather x5 -> x0, waiting for transfers between devices: 299 us -> none  [the longest x1 93.5 us: body(): lax.all_gather(w_up[layer_no], 'dp', axis=0, tiled=True)]
    psum x3 -> x0, waiting for transfers between devices: 87.2 us -> none  [the longest x1 38.4 us: backward_layer(): lax.psum(contract_cols(grad_gate_b, w_gate) + contract_cols(grad_up_b, w_...]
    all_gather x4 -> x0, blocking collectives: 84.4 us -> none  [the longest x1 23.3 us: body(): lax.all_gather(gain_attn[layer_no], 'dp', axis=0, tiled=True)]
    unnamed x1 -> x0, blocking collectives: 61 us -> none
    dot_general x7 -> x3, matrix products: 55.2 us -> 7.42 us  [contract_rows(): lax.dot_general(left, right, (((0,), (0,)), ((), ())), preferred_element_...]
    dot_general x13 -> x3, matrix products: 40.8 us -> 10.6 us  [the longest x1 4.23 us: fast_body(): feed_p = jnp.dot(hidden_act, w3[2], preferred_element_type=F32).astype(BF)]
  transfers between devices with their start and end apart: 15 -> 0, of which waited for: 13 -> 0; matrix products, arithmetic and copies ran while one was open for 6% -> 0% of each run, Pallas kernels for 0% -> 0%
where the time goes in v1:
time: 380 us; the launch traced here: 379 us
  Pallas kernels  323 us (85%)
  matrix products  28.9 us (8%)
  local copies, waits for them, and re-layouts  14.7 us (4%)
  other arithmetic  11.3 us (3%)
    pallas_call x1, Pallas kernels, back(): pl.pallas_call(back_kernel, name='back', out_shape=(jax.ShapeDtypeStruct(...  162 us
    pallas_call x1, Pallas kernels, front(): pl.pallas_call(front_kernel, name='front', out_shape=(jax.ShapeDtypeStruc...  161 us
    dot_general x3, matrix products, contract_cols(): lax.dot_general(left, right, (((1,), (1,)), ((), ())), preferred_element_...  10.9 us
    unnamed x24, local copies, waits for them, and re-layouts  10.4 us

profile of v1, /device:TPU:0, one launch (start us, length us, event | category | flops | bytes accessed | tf_op | source)
XLA Modules:
  0.0 379.2 jit_solution(2529367839499600570)
XLA Ops:
  0.7 0.1 pad.13.clone
  0.7 1.3 maximum_maximum_fusion.ga_l
  2.1 1.2 slice.42
  3.9 0.8 compare_select_fusion
  4.7 0.3 reduce-window.6
  5.1 0.2 slice_reduce_fusion
  5.2 0.2 reduce-window.9
  5.4 0.1 broadcast.77
  5.5 0.2 fusion.22
  5.7 0.7 copy.25.cos_t
  6.5 0.7 copy.26.sin_t
  7.2 1.5 fusion.21.mask
  8.7 160.7 %front.1 = (bf16[2048,1280]{1,0:T(8,128)(2,1)}, bf16[1024,2048]{1,0:T(8,128)(2,1)}, bf16[16,2048]{1,0:T(8,128)(2,1)}, bf16[3,704,2048]{2,1,0:T(8,128)(2,1)}, bf1...) custom-call(f32[176,2048]{1,0:T(8,128)} %resid.3, ...), custom_call_target="tpu_custom_call" | custom-call | tf_op jit(solution)/shard_map/front/pallas_call | solution.py:735
  169.4 0.0 copy-start.5
  169.4 0.0 copy-start.7
  169.4 5.3 %fusion.5 = f32[704,704]{1,0:T(8,128)S(1)} fusion(bf16[704,2048]{1,0:T(8,128)(2,1)} %get-tuple-element.32, bf16[3,704,2048]{2,1,0:T(8,128)(2,1)} %get-tuple-element.31), kind=kOutput, calls=%fused_computation.11 | convolution fusion | flops 2030043136 | bytes 7749632 | tf_op jit(solution)/shard_map/dot_general | solution.py:111
  174.7 0.0 copy-done.5
  174.7 0.7 copy-done.7
  175.4 0.0 copy-start.6
  175.4 2.4 fusion.11
  177.9 0.0 copy-done.6
  177.9 3.2 multiply_convert_fusion
  181.1 2.4 fusion.3
  183.5 3.9 %add_convert_fusion.dn_p = bf16[704,2048]{1,0:T(8,128)(2,1)} fusion(f32[704,2048]{1,0:T(8,128)S(1)} %fusion.3, bf16[704,704]{1,0:T(8,128)(2,1)S(1)} %get-tuple-element.73, bf16[3,704,2048]{2,1,0:T(8,128)(2,1)S(1)} %copy-done.5), kind=kOutput, calls=%fused_computation.1 | convolution fusion | flops 2032926720 | bytes 12615680 | tf_op jit(solution)/shard_map/dot_general | solution.py:1251
  187.4 4.2 %convolution_convert_fusion.3.feed_p = bf16[704,2048]{1,0:T(8,128)(2,1)} fusion(bf16[704,704]{1,0:T(8,128)(2,1)S(1)} %get-tuple-element.71, bf16[3,704,2048]{2,1,0:T(8,128)(2,1)S(1)} %copy-done.5), kind=kOutput, calls=%fused_computation.5 | convolution fusion | flops 2031484928 | bytes 6848512 | tf_op jit(solution)/shard_map/dot_general | solution.py:1248
  191.7 2.5 fusion.2
  194.1 2.5 fusion.1
  196.6 2.5 fusion
  199.1 4.0 %pad_maximum_fusion.g3_p = bf16[3,704,2048]{2,1,0:T(8,128)(2,1)} fusion(bf16[1,704,2048]{2,1,0:T(8,128)(2,1)S(1)} %fusion.2, bf16[1,704,2048]{2,1,0:T(8,128)(2,1)S(1)} %fusion.1, bf16[1,704,2048]{2,1,0:T(8,128)(2,1)S(1)} %fusion), kind=kLoop, calls=%fused_computation | loop fusion | flops 8650752 | bytes 17301504 | tf_op jit(solution)/shard_map/stack | solution.py:1253
  203.1 162.2 %back.1 = (f32[176,2048]{1,0:T(8,128)}, f32[176,2048]{1,0:T(8,128)}, bf16[3,2816,128]{2,1,0:T(8,128)(2,1)}, f32[1,128,1024]{2,1,0:T(8,128)}, f32[1,128,128]{2,1,...) custom-call(bf16[704,2048]{1,0:T(8,128)(2,1)} %add_convert_fusion.dn_p, ...), custom_call_target="tpu_custom_call" | custom-call | tf_op jit(solution)/shard_map/back/pallas_call | solution.py:1159
  365.2 1.3 fusion.25
  366.5 2.9 slice_convert_fusion
  369.4 1.5 copy.29
  371.0 0.0 copy-start
  371.0 1.5 copy.30
  372.5 0.0 copy-start.2
  372.5 0.0 copy-start.4
  372.5 0.0 copy-start.3
  372.5 0.0 copy-start.1
  372.5 2.7 copy.37
  375.2 0.0 copy-done
  375.2 1.1 copy.38
  376.3 0.0 copy-done.2
  376.3 0.8 copy.39
  377.1 0.0 copy-done.4
  377.1 0.6 copy.40
  377.8 0.0 copy-done.3
  377.8 0.6 copy.41
  378.4 0.0 copy-done.1
  378.4 0.8 copy.42
  (8 shorter events, 0.1 us)
Async XLA Ops:
  169.4 5.3 %copy-start.5 = (bf16[3,704,2048]{2,1,0:T(8,128)(2,1)S(1)}, bf16[3,704,2048]{2,1,0:T(8,128)(2,1)}, u32[]{:S(2)}) copy-start(bf16[3,704,2048]{2,1,0:T(8,128)(2,1)} %get-tuple-element.31) | copy-start | bytes 25952260
  169.4 6.0 %copy-start.7 = (bf16[704,2048]{1,0:T(8,128)(2,1)S(1)}, bf16[704,2048]{1,0:T(8,128)(2,1)}, u32[]{:S(2)}) copy-start(bf16[704,2048]{1,0:T(8,128)(2,1)} %get-tuple-element.30) | copy-start | bytes 8650756
  175.4 2.5 copy-start.6
  371.0 4.3 %copy-start = (f32[176,2048]{1,0:T(8,128)S(1)}, f32[176,2048]{1,0:T(8,128)}, u32[]{:S(2)}) copy-start(f32[176,2048]{1,0:T(8,128)} %get-tuple-element.94) | copy-start | bytes 4325380
  372.5 3.8 %copy-start.2 = (f32[1,128,1024]{2,1,0:T(8,128)S(1)}, f32[1,128,1024]{2,1,0:T(8,128)}, u32[]{:S(2)}) copy-start(f32[1,128,1024]{2,1,0:T(8,128)} %get-tuple-element.96) | copy-start | bytes 1572868
  372.5 4.6 %copy-start.4 = (f32[1,128,128]{2,1,0:T(8,128)S(1)}, f32[1,128,128]{2,1,0:T(8,128)}, u32[]{:S(2)}) copy-start(f32[1,128,128]{2,1,0:T(8,128)} %get-tuple-element.97) | copy-start | bytes 196612
  372.5 5.2 %copy-start.3 = (f32[1,128,128]{2,1,0:T(8,128)S(1)}, f32[1,128,128]{2,1,0:T(8,128)}, u32[]{:S(2)}) copy-start(f32[1,128,128]{2,1,0:T(8,128)} %get-tuple-element.98) | copy-start | bytes 196612
  372.5 5.9 %copy-start.1 = (f32[1,1024,128]{2,1,0:T(8,128)S(1)}, f32[1,1024,128]{2,1,0:T(8,128)}, u32[]{:S(2)}) copy-start(f32[1,1024,128]{2,1,0:T(8,128)} %get-tuple-element.99) | copy-start | bytes 1572868

commit v2 on v1

--- a/solution.py
+++ b/solution.py
@@ -1,5 +1,6 @@
 import jax
 import jax.numpy as jnp
+import numpy as np
 from jax import lax
 from jax.experimental import pallas as pl
 from jax.experimental.pallas import tpu as pltpu
@@ -489,14 +490,22 @@
         self.up, self.down = dev(z + 1, x, c, y), dev(z - 1, x, c, y)
         self.side, self.twin = dev(z, 1 - x, c, y), dev(z, x, 1 - c, y)
 
-    def start(self):
+    def start_z(self):
         z, wire = self.z, self.wire
         d = self.blk(rid(z, self.x, self.c))
         wire.send(self.own, d, self.s + z, self.r + z, self.up, z < ZN - 1)
         wire.send(self.own, d, self.s + 4 + z, self.r + z, self.down, z > 0)
+
+    def start_near(self):
+        z, wire = self.z, self.wire
+        d = self.blk(rid(z, self.x, self.c))
         wire.send(self.own, d, self.s + 8 + z, self.r + 4 + z, self.side)
         k = z * 2 + self.x
         wire.send(self.own, d, self.s + 12 + k, self.r + 8 + k, self.twin)
+
+    def start(self):
+        self.start_z()
+        self.start_near()
 
     def relay(self, s):
         z, wire = self.z, self.wire
@@ -528,20 +537,32 @@
 
 
 def front_kernel(
-    resid, wq_l, wk_l, wv_l, wo_l, ga_l, wg_l, wu_l, wd_l, cot, cos_t, sin_t, mask,
-    wqkv, wo, ga, w3, dres, n1, q, kv, ctx, mid, normed,
-    qkv_l, w3_l, dres_l, kx, vx, attn, part, nrm, ss, rs, ls,
+    resid_h, wq_l, wk_l, wv_l, wo_l, g1_l, g2_l, wg_h, wu_h, wd_h, cot_h, seg, freq,
+    wqkv, wo, ga, w3, dres, n1, q, kv, ctx, mid, normed, cos_t, sin_t, mask,
+    resid, wg_l, wu_l, cot, ga_l, qkv_l, w3_l, dres_l, kx, vx, attn, part, nrm, ss, rs, ls,
 ):
     z, x, c, y = place()
     units = w3.shape[1]
     seq, width = resid.shape
     q_width = q.shape[1]
     pairs = q_width // LANE
+    loads = [
+        pltpu.make_async_copy(cot_h, cot, ls.at[6]),
+        pltpu.make_async_copy(wg_h.at[0], wg_l, ls.at[7]),
+        pltpu.make_async_copy(wu_h.at[0], wu_l, ls.at[8]),
+        pltpu.make_async_copy(wd_h.at[0], w3_l.at[2], ls.at[9]),
+        pltpu.make_async_copy(resid_h, resid, ls.at[10]),
+    ]
+    for cp in loads:
+        cp.start()
     wire = Wire(ss, rs)
     side, twin, other = dev(z, 1 - x, c, y), dev(z, x, 1 - c, y), dev(z, x, c, 1 - y)
     qkv_l[:, pl.ds(0, q_width)] = wq_l[0]
     qkv_l[:, pl.ds(q_width, LANE)] = wk_l[0]
     qkv_l[:, pl.ds(q_width + LANE, LANE)] = wv_l[0]
+    row = lax.broadcasted_iota(jnp.int32, (16, LANE), 0)
+    two = jnp.where(row == 0, g1_l[...].astype(F32), g2_l[...].astype(F32))
+    ga_l[...] = jnp.where(row < 2, two, 0.0).astype(BF)
     greet(all_peers(z, x, c, y))
 
     def qkv_blk(r):
@@ -575,46 +596,15 @@
     def round_cot(r):
         dres_l[r, :] = cot[r, :].astype(BF)
 
-    by_rows(seq, 16, round_cot)
-    for s in (1, 2, 3):
-        t_ga.relay(s)
-    for s in (0, 1, 2, 3):
-        t_ga.across(s)
-    t_qkv.relay(1)
-    t_qkv.across(0)
-    t_ga.finish()
-    own[2].wait()
-    gain_one = ga[pl.ds(0, 8), :].astype(F32)[0:1]
-    gain_two = ga[pl.ds(0, 8), :].astype(F32)[1:2]
-
-    def norm_one(r):
-        v = resid[r, :]
-        recip = lax.rsqrt(jnp.mean(v * v, axis=-1, keepdims=True) + epsilon)
-        n1[r, :] = (v * recip * gain_one).astype(BF)
-
-    by_rows(seq, 16, norm_one)
-    t_qkv.relay(2)
-    t_qkv.across(1)
-    t_qkv.relay(3)
-    t_wo.start()
-
     def turn(i, carry):
         cut = lanes(i)
         w3_l[0, pl.ds(pl.multiple_of(i * LANE, LANE), LANE), :] = (
-            wg_l[0, :, cut].astype(F32).T.astype(BF)
+            wg_l[:, cut].astype(F32).T.astype(BF)
         )
         w3_l[1, pl.ds(pl.multiple_of(i * LANE, LANE), LANE), :] = (
-            wu_l[0, :, cut].astype(F32).T.astype(BF)
+            wu_l[:, cut].astype(F32).T.astype(BF)
         )
         return carry
-
-    lax.fori_loop(0, w3_l.shape[1] // LANE, turn, 0)
-    by_rows(w3_l.shape[1], 64, lambda r: w3_l.at[2].__setitem__((r, slice(None)), wd_l[0, r, :]))
-    t_qkv.across(2)
-    t_qkv.across(3)
-    t_wo.relay(1)
-    t_qkv.finish()
-    own[0].wait()
 
     def turned(v):
         return v * cos_t[...] + swap_halves(v) * sin_t[...]
@@ -624,17 +614,6 @@
         for h in (0, 1):
             q[:, lanes(2 * j + h)] = turned(acc[:, h * LANE : (h + 1) * LANE]).astype(BF)
         return carry
-
-    lax.fori_loop(0, pairs // 2, q_tile, 0)
-    acc = dot_nn(n1[...], wqkv[:, pl.ds(q_width, 2 * LANE)])
-    key = turned(acc[:, :LANE]).astype(BF)
-    val = acc[:, LANE:].astype(BF)
-    kv[:, pl.ds(0, LANE)] = key
-    kv[:, pl.ds(LANE, LANE)] = val
-    spread_pair(kx, key.astype(F32))
-    spread_pair(vx, val.astype(F32))
-    t_wo.relay(2)
-    t_wo.across(0)
 
     def pair(p, carry):
         qp = q[:, lanes(p)]
@@ -649,22 +628,76 @@
         ctx[:, lanes(p)] = out.astype(BF)
         return carry
 
-    lax.fori_loop(0, pairs // 2, pair, 0)
-    t_wo.relay(3)
+    ids = jnp.broadcast_to(seg[...].astype(F32), (seq, seq))
+    own_id = lax.broadcasted_iota(jnp.int32, (seq, seq), 0)
+    key_id = lax.broadcasted_iota(jnp.int32, (seq, seq), 1)
+    mine_id = jnp.sum(jnp.where(own_id == key_id, ids, 0.0), axis=1, keepdims=True)
+    seen = jnp.where((ids == mine_id) & (key_id <= own_id), 1.0, 0.0)
+    mask[...] = seen
+    angles = (jnp.sum(seen, axis=1, keepdims=True) - 1.0) * freq[...]
+    lane = lax.broadcasted_iota(jnp.int32, (seq, LANE), 1)
+    cos_t[...] = jnp.cos(angles)
+    sin_t[...] = jnp.where(lane % HD < HD // 2, -1.0, 1.0) * jnp.sin(angles)
+    loads[0].wait()
+    by_rows(seq, 16, round_cot)
+    t_ga.relay(1)
+    t_qkv.relay(1)
+    t_ga.across(0)
+    t_qkv.across(0)
+    t_ga.relay(2)
+    t_qkv.relay(2)
+    t_wo.start_z()
+    for cp in loads[1:]:
+        cp.wait()
+    lax.fori_loop(0, w3_l.shape[1] // LANE, turn, 0)
+    t_ga.across(1)
+    t_qkv.across(1)
+    t_ga.relay(3)
+    t_qkv.relay(3)
+    t_wo.start_near()
+    t_ga.across(2)
+    t_ga.across(3)
+    t_ga.finish()
+    own[2].wait()
+    gain_one = ga[pl.ds(0, 8), :].astype(F32)[0:1]
+    gain_two = ga[pl.ds(0, 8), :].astype(F32)[1:2]
+
+    def norm_one(r):
+        v = resid[r, :]
+        recip = lax.rsqrt(jnp.mean(v * v, axis=-1, keepdims=True) + epsilon)
+        n1[r, :] = (v * recip * gain_one).astype(BF)
+
+    by_rows(seq, 16, norm_one)
+    t_wo.relay(1)
+    t_qkv.across(2)
+    t_wo.relay(2)
+    l_dres.start()
     for d in (2, 1, 3):
         zt = (z + d) % ZN
         wire.send(w3_l.at[:, rows(zt, units), :], ffn(mine), 60 + d - 1, 48 + z, dev(zt, x, c, y))
+    t_qkv.across(3)
+    t_qkv.finish()
+    own[0].wait()
+    lax.fori_loop(0, pairs // 2, q_tile, 0)
+    acc = dot_nn(n1[...], wqkv[:, pl.ds(q_width, 2 * LANE)])
+    key = turned(acc[:, :LANE]).astype(BF)
+    val = acc[:, LANE:].astype(BF)
+    kv[:, pl.ds(0, LANE)] = key
+    kv[:, pl.ds(LANE, LANE)] = val
+    spread_pair(kx, key.astype(F32))
+    spread_pair(vx, val.astype(F32))
+    t_wo.across(0)
+    t_wo.relay(3)
     mine3 = w3_l.at[:, rows(z, units), :]
     wire.send(mine3, ffn(mine), 64 + z, 52 + z, side)
     wire.send(mine3, ffn(mine), 68 + z * 2 + x, 56 + z * 2 + x, twin)
-    l_dres.start()
     own += [
         pltpu.make_async_copy(mine3, ffn(mine), ls.at[3]),
         pltpu.make_async_copy(dres_l, dres.at[rows(z, seq), :], ls.at[4]),
     ]
     own[3].start()
     own[4].start()
-    lax.fori_loop(pairs // 2, pairs, pair, 0)
+    lax.fori_loop(0, pairs, pair, 0)
     for s in (1, 2, 3):
         t_wo.across(s)
     t_wo.finish()
@@ -677,7 +710,6 @@
 
     lax.fori_loop(0, width // (2 * LANE), out_tile, 0)
     wire.send(attn, part, 100, 80, other)
-    l_dres.relay(1)
 
     def ffn_in(d):
         o = (z + ZN - d) % ZN
@@ -693,23 +725,23 @@
         k = o * 2 + 1 - x
         wire.send(b, b, 68 + k, 56 + k, twin)
 
-    ffn_in(2)
-    wire.arrived(part, 80, other)
-
     def second(r):
         m = resid[r, :] + (attn[r, :].astype(F32) + part[r, :].astype(F32))
         mid[r, :] = m
         recip = lax.rsqrt(jnp.mean(m * m, axis=-1, keepdims=True) + epsilon)
         nrm[r, :] = (m * recip * gain_two).astype(BF)
 
+    l_dres.relay(1)
+    ffn_in(2)
+    wire.arrived(part, 80, other)
     by_rows(seq, 16, second)
     l_norm.start()
     own.append(pltpu.make_async_copy(nrm, normed.at[rows(z, seq), :], ls.at[5]))
     own[5].start()
+    l_dres.relay(2)
     ffn_in(1)
-    l_dres.relay(2)
+    ffn_across(0)
     l_norm.relay(1)
-    ffn_across(0)
     ffn_in(3)
     l_dres.relay(3)
     l_norm.relay(2)
@@ -726,12 +758,15 @@
         cp.wait()
 
 
-def front(resid, w_query, w_key, w_value, w_out, gains, w_gate, w_up, w_down, cot, cos_t, sin_t, mask):
+def front(resid, w_query, w_key, w_value, w_out, g1, g2, w_gate, w_up, w_down, cot, seg):
     seq, width = resid.shape
     q_width, out_rows = w_query.shape[2], w_out.shape[1]
     total = q_width + 2 * LANE
     units = w_gate.shape[2] // ZN
     pair_shape = (4, seq, LANE)
+    freq = rope_base ** (-(np.arange(LANE) % (HD // 2)) * 2.0 / HD)
+    freq = jnp.asarray(freq[None].astype(np.float32))
+    vm, hb = vm_spec(), any_spec()
     return pl.pallas_call(
         front_kernel,
         name="front",
@@ -747,10 +782,18 @@
             jax.ShapeDtypeStruct((seq, q_width), BF),
             jax.ShapeDtypeStruct((seq, width), F32),
             jax.ShapeDtypeStruct((seq * ZN, width), BF),
+            jax.ShapeDtypeStruct((seq, LANE), F32),
+            jax.ShapeDtypeStruct((seq, LANE), F32),
+            jax.ShapeDtypeStruct((seq, seq), F32),
         ),
-        in_specs=[vm_spec()] * 13,
-        out_specs=[vm_spec()] * 3 + [any_spec()] * 2 + [vm_spec()] * 5 + [any_spec()],
+        in_specs=[hb] + [vm] * 6 + [hb] * 4 + [vm] * 2,
+        out_specs=[vm] * 3 + [hb] * 2 + [vm] * 5 + [hb] + [vm] * 3,
         scratch_shapes=[
+            pltpu.VMEM((seq, width), F32),
+            pltpu.VMEM((LANE, units * ZN), BF),
+            pltpu.VMEM((LANE, units * ZN), BF),
+            pltpu.VMEM((seq, width), F32),
+            pltpu.VMEM((16, LANE), BF),
             pltpu.VMEM((LANE, total), BF),
             pltpu.VMEM((3, units * ZN, LANE), BF),
             pltpu.VMEM((seq, width), BF),
@@ -761,10 +804,10 @@
             pltpu.VMEM((seq, width), BF),
             sems(101),
             sems(81),
-            sems(6),
+            sems(11),
         ],
         compiler_params=params(0),
-    )(resid, w_query, w_key, w_value, w_out, gains, w_gate, w_up, w_down, cot, cos_t, sin_t, mask)
+    )(resid, w_query, w_key, w_value, w_out, g1, g2, w_gate, w_up, w_down, cot, seg, freq)
 
 
 def add_into(dst, src, height, step):
@@ -834,11 +877,29 @@
         self.wire.arrived(self.cin.at[k], self.r + k, self.twin)
         add_into(self.cin.at[k], self.part(k * 2 + self.c), self.height, self.step)
 
+    def from_twin_if(self, k, cond):
+        self.wire.arrived(self.cin.at[k], self.r + k, self.twin, cond)
+
+        @pl.when(cond)
+        def _():
+            add_into(self.cin.at[k], self.part(k * 2 + self.c), self.height, self.step)
+
+    def across_one(self, o, cond=None):
+        k = o * 2 + 1 - self.x
+        if cond is None:
+            self.from_twin(k)
+        else:
+            self.from_twin_if(k, cond)
+        self.wire.send(
+            self.cin.at[k], self.xin.at[o], self.s + 8 + o, self.r + 8 + o, self.side, cond
+        )
+
     def across(self):
-        for o in self.order():
-            k = o * 2 + 1 - self.x
-            self.from_twin(k)
-            self.wire.send(self.cin.at[k], self.xin.at[o], self.s + 8 + o, self.r + 8 + o, self.side)
+        z = self.z
+        for t in (3, 2, 1):
+            self.across_one(z + t, z + t < ZN)
+            self.across_one(z - t, z >= t)
+        self.across_one(z)
 
     def stay(self):
         for o in self.order():
@@ -861,9 +922,10 @@
 
 
 def back_kernel(
-    dn_p, feed_p, g3_p, mid, cot, resid, ga, n1, q, kv, ctx, wqkv, wo, cos_t, sin_t, mask,
-    hidden, grad_in, g3, gq_out, gk_out, gv_out, go_out, gains_out,
-    fown, yin, zin, gbuf, cin, xin, gq_p, go_p, gp, qc, qx, qz, oc, ox, oz, gc, gx, gz,
+    dn_p, feed_p, g3_p, wqkv, mid_h, cot_h, resid_h, ga_h, n1_h, q_h, kv_h, ctx_h, wo_h, cos_h,
+    sin_h, mask_h,
+    feed_out, grad_out, g3, gq_out, go_out, gains_out,
+    mid, cot, resid, ga, n1, q, kv, ctx, wo, cos_t, sin_t, mask, grad_in, fown, yin, zin, gbuf, cin, xin, gq_p, go_p, gp, qc, qx, qz, oc, ox, oz, gc, gx, gz,
     dn, feed, mid_b, dctx, dqkv, dn1, dn1_o, kx, vx, kacc, vacc, wbuf, gs, gr, ss, rs, ls,
 ):
     z, x, c, y = place()
@@ -887,6 +949,15 @@
         wire.send(s, yin.at[k, z], k * 4 + z, k * 4 + z, other)
 
     y_out(dn_p, 0)
+
+    def own_half(k, o):
+        src = (dn_p, feed_p)[k]
+        return pltpu.make_async_copy(
+            src.at[rows(o, seq), lanes(y, half)], fown.at[k, o], ls.at[2 + k * 4 + o]
+        )
+
+    for o in range(ZN):
+        own_half(0, o).start()
     for k in range(8):
         wire.send(g3_p.at[:, :, lanes(k * 2 + 1 - c)], cin.at[k], 26 + k, 20 + k, twin)
     ks = [o * 2 + 1 - x for o in ring] + [o * 2 + x for o in ring]
@@ -894,11 +965,6 @@
     def load(i):
         return pltpu.make_async_copy(
             g3_p.at[:, :, lanes(ks[i] * 2 + c)], gbuf.at[i % 2], ls.at[i % 2]
-        )
-
-    def own_half(o):
-        return pltpu.make_async_copy(
-            feed_p.at[rows(o, seq), lanes(y, half)], fown.at[o], ls.at[2 + o]
         )
 
     def add3(dst, src):
@@ -915,9 +981,18 @@
         if i < 4:
             o = ring[i]
             wire.send(cin.at[ks[i]], xin.at[o], 34 + o, 28 + o, side)
+    pairs_in = (
+        (wo_h, wo), (ga_h, ga), (kv_h, kv), (mask_h, mask), (mid_h, mid), (cot_h, cot), (n1_h, n1),
+        (q_h, q), (ctx_h, ctx), (cos_h, cos_t), (sin_h, sin_t), (resid_h, resid),
+    )
+    inward = [
+        pltpu.make_async_copy(a, b, ls.at[13 + i]) for i, (a, b) in enumerate(pairs_in)
+    ]
+    for cp in inward:
+        cp.start()
     for o in range(ZN):
-        own_half(o).start()
-
+        own_half(1, o).start()
+        own_half(0, o).wait()
     def chain_of(k):
         return Chain(
             wire, lambda o: yin.at[k, o], lambda s: zin.at[k, s], seq, 16, 8 + k * 8, 8 + k * 5
@@ -928,11 +1003,7 @@
 
         @pl.when(cond)
         def _():
-            def one(r):
-                mine = dn_p[pl.ds(pl.multiple_of(o * seq, 16) + r.start, 16), lanes(y, half)]
-                yin[0, o, r, :] = (yin[0, o, r, :].astype(F32) + mine.astype(F32)).astype(BF)
-
-            by_rows(seq, 16, one)
+            add_into(yin.at[0, o], fown.at[0, o], seq, 16)
 
     line = chain_of(0)
     for t in (3, 2, 1):
@@ -956,10 +1027,12 @@
         if d:
             wire.send(xin.at[o], g3.at[:, rows(z, units), :], 38 + d - 1, 32 + z, dev(o, x, c, y))
         else:
-            pltpu.make_async_copy(xin.at[o], g3.at[:, rows(z, units), :], ls.at[6]).start()
+            pltpu.make_async_copy(xin.at[o], g3.at[:, rows(z, units), :], ls.at[10]).start()
 
     ffn_z(0)
     ffn_z(1)
+    for cp in inward:
+        cp.wait()
     spread_pair(kx, kv[:, pl.ds(0, LANE)].astype(F32))
     spread_pair(vx, kv[:, pl.ds(LANE, LANE)].astype(F32))
     kacc[...] = jnp.zeros_like(kacc)
@@ -1046,7 +1119,7 @@
 
     def w_tile(j, slot):
         r = pl.ds(pl.multiple_of(j * 2 * LANE, 2 * LANE), 2 * LANE)
-        return pltpu.make_async_copy(wqkv.at[r, :], wbuf.at[slot], ls.at[7 + slot])
+        return pltpu.make_async_copy(wqkv.at[r, :], wbuf.at[slot], ls.at[11 + slot])
 
     w_tile(0, 0).start()
 
@@ -1058,6 +1131,7 @@
 
     lax.fori_loop(0, width // LANE, in_grad, 0)
     f_q.to_twin()
+    f_q.across()
     tiles = width // (2 * LANE)
     for j in range(tiles):
         if j + 1 < tiles:
@@ -1065,7 +1139,6 @@
         w_tile(j, j % 2).wait()
         dn1[:, pl.ds(j * 2 * LANE, 2 * LANE)] = dot_nt(dqkv[...], wbuf[j % 2]).astype(BF)
     wire.send(dn1, dn1_o, 101, 87, other)
-    f_q.across()
 
     def gain_part(r):
         v = resid[r, :]
@@ -1081,14 +1154,14 @@
         f_o.outward(t)
 
     for o in range(ZN):
-        own_half(o).wait()
+        own_half(1, o).wait()
 
     def feed_ready(o, cond):
         wire.arrived(yin.at[1, o], 4 + o, other, cond)
 
         @pl.when(cond)
         def _():
-            add_into(yin.at[1, o], fown.at[o], seq, 16)
+            add_into(yin.at[1, o], fown.at[1, o], seq, 16)
 
     line = chain_of(1)
     for t in (3, 2, 1):
@@ -1118,22 +1191,20 @@
         grad_in[r, :] += d
 
     by_rows(seq, 16, norm_one)
+    outward = [pltpu.make_async_copy(grad_in, grad_out, ls.at[25])]
+    outward[0].start()
     done = f_o.home()
-    by_rows(out_rows, 64, lambda r: go_out.at[0].__setitem__((r, slice(None)), done[r, :].astype(F32)))
+    outward.append(pltpu.make_async_copy(done, go_out, ls.at[26]))
+    outward[1].start()
     mine = f_g.home()
     gs[...] = mine[...]
     wire.send(gs, gr, 102, 88, other)
     got = f_q.home()
-    cut_k, cut_v = pl.ds(q_width, LANE), pl.ds(q_width + LANE, LANE)
-    gq_out[0] = got[:, pl.ds(0, q_width)].astype(F32)
-    gk_out[0] = got[:, cut_k].astype(F32)
-    gv_out[0] = got[:, cut_v].astype(F32)
+    outward.append(pltpu.make_async_copy(got, gq_out, ls.at[27]))
+    outward[2].start()
     wire.arrived(feed.at[:, lanes(1 - y, half)], 19, other)
-
-    def last(r):
-        hidden[r, :] = mid[r, :] + feed[r, :].astype(F32)
-
-    by_rows(seq, 16, last)
+    outward.append(pltpu.make_async_copy(feed, feed_out, ls.at[28]))
+    outward[3].start()
     wire.arrived(gr, 88, other)
     first = jnp.sum(gs[pl.ds(0, 8), :] + gr[pl.ds(0, 8), :], axis=0, keepdims=True)
     second = jnp.sum(gs[pl.ds(8, 8), :], axis=0, keepdims=True)
@@ -1143,10 +1214,12 @@
         o = (z + ZN - d) % ZN
         wire.arrived(g3.at[:, rows(o, units), :], 32 + o, dev(o, x, c, y))
     wire.drain()
-    pltpu.make_async_copy(xin.at[z], g3.at[:, rows(z, units), :], ls.at[6]).wait()
-
-
-def back(dn_p, feed_p, g3_p, mid, cot, resid, ga, n1, q, kv, ctx, wqkv, wo, cos_t, sin_t, mask):
+    pltpu.make_async_copy(xin.at[z], g3.at[:, rows(z, units), :], ls.at[10]).wait()
+    for cp in outward:
+        cp.wait()
+
+
+def back(dn_p, feed_p, g3_p, wqkv, mid, cot, resid, ga, n1, q, kv, ctx, wo, cos_t, sin_t, mask):
     seq, width = mid.shape
     units = g3_p.shape[1]
     q_width, total = q.shape[1], wqkv.shape[1]
@@ -1156,23 +1229,24 @@
     def vm(*shape, dtype=BF):
         return pltpu.VMEM(shape, dtype)
 
+    held = (mid, cot, resid, ga, n1, q, kv, ctx, wo, cos_t, sin_t, mask)
     return pl.pallas_call(
         back_kernel,
         name="back",
         out_shape=(
-            jax.ShapeDtypeStruct((seq, width), F32),
+            jax.ShapeDtypeStruct((seq, width), BF),
             jax.ShapeDtypeStruct((seq, width), F32),
             jax.ShapeDtypeStruct((3, units * ZN, LANE), BF),
-            jax.ShapeDtypeStruct((1, LANE, q_width), F32),
-            jax.ShapeDtypeStruct((1, LANE, LANE), F32),
-            jax.ShapeDtypeStruct((1, LANE, LANE), F32),
-            jax.ShapeDtypeStruct((1, out_rows, LANE), F32),
+            jax.ShapeDtypeStruct((LANE, total), BF),
+            jax.ShapeDtypeStruct((out_rows, LANE), BF),
             jax.ShapeDtypeStruct((8, LANE), F32),
         ),
-        in_specs=[vm_spec()] + [any_spec()] * 2 + [vm_spec()] * 8 + [any_spec()] + [vm_spec()] * 4,
-        out_specs=[vm_spec()] * 2 + [any_spec()] + [vm_spec()] * 5,
-        scratch_shapes=[
-            vm(ZN, seq, half),
+        in_specs=[any_spec()] * 16,
+        out_specs=[any_spec()] * 5 + [vm_spec()],
+        scratch_shapes=[vm(*a.shape, dtype=a.dtype) for a in held]
+        + [
+            vm(seq, width, dtype=F32),
+            vm(2, ZN, seq, half),
             vm(2, ZN, seq, half),
             vm(2, 5, seq, half),
             vm(2, 3, units, LANE),
@@ -1206,12 +1280,118 @@
             vm(16, LANE, dtype=F32),
             sems(103),
             sems(89),
-            sems(9),
+            sems(29),
         ],
         compiler_params=pltpu.CompilerParams(
             collective_id=1, has_side_effects=True, vmem_limit_bytes=67043328
         ),
-    )(dn_p, feed_p, g3_p, mid, cot, resid, ga, n1, q, kv, ctx, wqkv, wo, cos_t, sin_t, mask)
+    )(dn_p, feed_p, g3_p, wqkv, *held)
+
+
+def finish_kernel(
+    mid_h, feed_h, grad_h, g3_h, gq_h, go_h, gains,
+    hidden, grad_in, wg, wu, wd, wq, wk, wv, wo, first, second,
+    mid, feed, grad, g3, gq, go, tg, td, tq, to, ls,
+):
+    q_width = wq.shape[2]
+    units = td.shape[0]
+    into = [
+        pltpu.make_async_copy(a, b, ls.at[i])
+        for i, (a, b) in enumerate(
+            ((g3_h, g3), (mid_h, mid), (feed_h, feed), (gq_h, gq), (go_h, go), (grad_h, grad))
+        )
+    ]
+    for cp in into:
+        cp.start()
+    first[...] = gains[pl.ds(0, 1), :]
+    second[...] = gains[pl.ds(1, 1), :]
+    out = []
+
+    def put(src, dst):
+        cp = pltpu.make_async_copy(src, dst, ls.at[6 + len(out)])
+        cp.start()
+        out.append(cp)
+
+    into[0].wait()
+    for m, dst in ((0, wg), (1, wu)):
+
+        def turn(i, carry):
+            r = pl.ds(pl.multiple_of(i * LANE, LANE), LANE)
+            tg[m, :, lanes(i)] = g3[m, r, :].astype(F32).T
+            return carry
+
+        lax.fori_loop(0, units // LANE, turn, 0)
+        put(tg.at[m], dst.at[0])
+
+    def wide(r):
+        td[r, :] = g3[2, r, :].astype(F32)
+
+    by_rows(units, 64, wide)
+    put(td, wd.at[0])
+    into[1].wait()
+    into[2].wait()
+
+    def total(r):
+        mid[r, :] += feed[r, :].astype(F32)
+
+    by_rows(mid.shape[0], 16, total)
+    put(mid, hidden)
+    into[3].wait()
+
+    def wide_q(r):
+        tq[r, :] = gq[r, :].astype(F32)
+
+    by_rows(LANE, 16, wide_q)
+    put(tq.at[:, pl.ds(0, q_width)], wq.at[0])
+    put(tq.at[:, pl.ds(q_width, LANE)], wk.at[0])
+    put(tq.at[:, pl.ds(q_width + LANE, LANE)], wv.at[0])
+    into[4].wait()
+
+    def wide_o(r):
+        to[r, :] = go[r, :].astype(F32)
+
+    by_rows(to.shape[0], 64, wide_o)
+    put(to, wo.at[0])
+    into[5].wait()
+    put(grad, grad_in)
+    for cp in out:
+        cp.wait()
+
+
+def finish(mid, feed, grad, g3, gq, go, gains):
+    seq, width = mid.shape
+    units = g3.shape[1]
+    q_width = gq.shape[1] - 2 * LANE
+    f32 = lambda *shape: jax.ShapeDtypeStruct(shape, F32)
+    ins = (mid, feed, grad, g3, gq, go)
+    return pl.pallas_call(
+        finish_kernel,
+        name="finish",
+        out_shape=(
+            f32(seq, width),
+            f32(seq, width),
+            f32(1, LANE, units),
+            f32(1, LANE, units),
+            f32(1, units, LANE),
+            f32(1, LANE, q_width),
+            f32(1, LANE, LANE),
+            f32(1, LANE, LANE),
+            f32(1, go.shape[0], LANE),
+            f32(1, LANE),
+            f32(1, LANE),
+        ),
+        in_specs=[any_spec()] * 6 + [vm_spec()],
+        out_specs=[any_spec()] * 9 + [vm_spec()] * 2,
+        scratch_shapes=[pltpu.VMEM(a.shape, a.dtype) for a in ins]
+        + [
+            pltpu.VMEM((2, LANE, units), F32),
+            pltpu.VMEM((units, LANE), F32),
+            pltpu.VMEM(gq.shape, F32),
+            pltpu.VMEM(go.shape, F32),
+            sems(15),
+        ],
+        compiler_params=pltpu.CompilerParams(vmem_limit_bytes=67043328),
+    )(*ins, gains)
 
 
 def fast_body(
@@ -1228,15 +1408,10 @@
     w_down,
     cotangent,
 ):
-    cos_t, sin_t = rope_tables(segment_positions(segment_ids))
-    cos_w = jnp.tile(cos_t[0], (1, 4))
-    sin_w = jnp.tile(jnp.concatenate([-sin_t[0], sin_t[0]], axis=1), (1, 2))
-    mask = attention_mask(segment_ids)[0, 0, 0].astype(F32)
-    gains = jnp.concatenate([gain_attn, gain_ffn, jnp.zeros((14, LANE), BF)], axis=0)
     resid = hidden_in
-    wqkv, wo, ga, w3, dres_all, n1, q, kv, ctx, middle, normed_all = front(
-        resid, w_query, w_key, w_value, w_out, gains, w_gate, w_up, w_down, cotangent,
-        cos_w, sin_w, mask,
+    wqkv, wo, ga, w3, dres_all, n1, q, kv, ctx, middle, normed_all, cos_w, sin_w, mask = front(
+        resid, w_query, w_key, w_value, w_out, gain_attn, gain_ffn, w_gate, w_up, w_down,
+        cotangent, segment_ids,
     )
     gate = contract_cols(normed_all, w3[0])
     up_proj = contract_cols(normed_all, w3[1])
@@ -1257,22 +1432,25 @@
             contract_rows(hidden_act, dres_all).astype(BF),
         ]
     )
-    hidden_out, grad_input, g3, gq, gk, gv, go, gains_g = back(
-        dn_p, feed_p, g3_p, middle, cotangent, resid, ga, n1, q, kv, ctx, wqkv, wo,
+    feed, grad_b, g3, gq, go, gains_g = back(
+        dn_p, feed_p, g3_p, wqkv, middle, cotangent, resid, ga, n1, q, kv, ctx, wo,
         cos_w, sin_w, mask,
+    )
+    hidden_out, grad_input, wg, wu, wd, wq, wk, wv, wo_g, first, second = finish(
+        middle, feed, grad_b, g3, gq, go, gains_g
     )
     return (
         hidden_out,
         grad_input,
-        gains_g[0:1],
-        gq,
-        gk,
-        gv,
-        go,
-        gains_g[1:2],
-        g3[0].T.astype(F32)[None],
-        g3[1].T.astype(F32)[None],
-        g3[2].astype(F32)[None],
+        first,
+        wq,
+        wk,
+        wv,
+        wo_g,
+        second,
+        wg,
+        wu,
+        wd,
     )
 
 

time: 380 us -> 349 us (0.918)
  local copies, waits for them, and re-layouts: 14.7 us -> 0.7 us
  Pallas kernels: 323 us -> 314 us
  other arithmetic: 11.3 us -> 3.95 us
    pallas_call x1, Pallas kernels: 161 us -> 149 us  [front(): pl.pallas_call(front_kernel, name='front', out_shape=(jax.ShapeDtypeStruc...]
    pallas_call x0 -> x1, Pallas kernels: none -> 10.3 us  [finish(): pl.pallas_call(finish_kernel, name='finish', out_shape=(f32(seq, width),...]
    unnamed x24 -> x6, local copies, waits for them, and re-layouts: 10.4 us -> 0.7 us
    pallas_call x1, Pallas kernels: 162 us -> 155 us  [back(): pl.pallas_call(back_kernel, name='back', out_shape=(jax.ShapeDtypeStruct(...]
    convert_element_type x3 -> x0, other arithmetic: 4.45 us -> none  [the longest x1 2.92 us: fast_body(): g3[2].astype(F32)[None]]
where the time goes in v2:
time: 349 us
  Pallas kernels  314 us (90%)
  matrix products  28.9 us (8%)
  other arithmetic  3.95 us (1%)
    pallas_call x1, Pallas kernels, back(): pl.pallas_call(back_kernel, name='back', out_shape=(jax.ShapeDtypeStruct(...  155 us
    pallas_call x1, Pallas kernels, front(): pl.pallas_call(front_kernel, name='front', out_shape=(jax.ShapeDtypeStruc...  149 us
    dot_general x3, matrix products, contract_cols(): lax.dot_general(left, right, (((1,), (1,)), ((), ())), preferred_element_...  10.9 us
    pallas_call x1, Pallas kernels, finish(): pl.pallas_call(finish_kernel, name='finish', out_shape=(f32(seq, width),...  10.3 us
    dot_general x3, matrix products, contract_rows(): lax.dot_general(left, right, (((0,), (0,)), ((), ())), preferred_element_...  7.42 us

profile of v2, /device:TPU:0, one launch (start us, length us, event | category | flops | bytes accessed | tf_op | source)
XLA Modules:
  0.0 348.6 jit_solution(5975986369320475666)
XLA Ops:
  0.6 148.9 %front.1 = (bf16[2048,1280]{1,0:T(8,128)(2,1)}, bf16[1024,2048]{1,0:T(8,128)(2,1)}, bf16[16,2048]{1,0:T(8,128)(2,1)}, bf16[3,704,2048]{2,1,0:T(8,128)(2,1)}, bf1...) custom-call(f32[176,2048]{1,0:T(8,128)} %resid_h.3, ...), custom_call_target="tpu_custom_call" | custom-call | tf_op jit(solution)/shard_map/front/pallas_call | solution.py:770
  149.6 0.0 copy-start
  149.6 0.0 copy-start.2
  149.6 5.3 %fusion.5 = f32[704,704]{1,0:T(8,128)S(1)} fusion(bf16[704,2048]{1,0:T(8,128)(2,1)} %get-tuple-element.45, bf16[3,704,2048]{2,1,0:T(8,128)(2,1)} %get-tuple-element.44), kind=kOutput, calls=%fused_computation.11 | convolution fusion | flops 2030043136 | bytes 7749632 | tf_op jit(solution)/shard_map/dot_general | solution.py:112
  154.9 0.0 copy-done
  154.9 0.7 copy-done.2
  155.6 0.0 copy-start.1
  155.6 2.4 fusion.11
  158.0 0.0 copy-done.1
  158.0 3.2 multiply_convert_fusion
  161.2 2.4 fusion.3
  163.6 4.0 %add_convert_fusion.dn_p = bf16[704,2048]{1,0:T(8,128)(2,1)} fusion(f32[704,2048]{1,0:T(8,128)S(1)} %fusion.3, bf16[704,704]{1,0:T(8,128)(2,1)S(1)} %get-tuple-element.75, bf16[3,704,2048]{2,1,0:T(8,128)(2,1)S(1)} %copy-done), kind=kOutput, calls=%fused_computation.1 | convolution fusion | flops 2032926720 | bytes 12615680 | tf_op jit(solution)/shard_map/dot_general | solution.py:1426
  167.6 4.2 %convolution_convert_fusion.3.feed_p = bf16[704,2048]{1,0:T(8,128)(2,1)} fusion(bf16[704,704]{1,0:T(8,128)(2,1)S(1)} %get-tuple-element.73, bf16[3,704,2048]{2,1,0:T(8,128)(2,1)S(1)} %copy-done), kind=kOutput, calls=%fused_computation.5 | convolution fusion | flops 2031484928 | bytes 6848512 | tf_op jit(solution)/shard_map/dot_general | solution.py:1423
  171.8 2.5 fusion.2
  174.3 2.5 fusion.1
  176.8 2.5 fusion
  179.3 3.9 %pad_maximum_fusion.g3_p = bf16[3,704,2048]{2,1,0:T(8,128)(2,1)} fusion(bf16[1,704,2048]{2,1,0:T(8,128)(2,1)S(1)} %fusion.2, bf16[1,704,2048]{2,1,0:T(8,128)(2,1)S(1)} %fusion.1, bf16[1,704,2048]{2,1,0:T(8,128)(2,1)S(1)} %fusion), kind=kLoop, calls=%fused_computation | loop fusion | flops 8650752 | bytes 17301504 | tf_op jit(solution)/shard_map/stack | solution.py:1428
  183.2 154.9 %back.1 = (bf16[176,2048]{1,0:T(8,128)(2,1)}, f32[176,2048]{1,0:T(8,128)}, bf16[3,2816,128]{2,1,0:T(8,128)(2,1)}, bf16[128,1280]{1,0:T(8,128)(2,1)}, bf16[1024,128]{1,0:T(8,128)(2,1)}, /*index=5*/f32[8,128]{1,0:T(8,128)}) custom-call(bf16[704,2048]{1,0:T(8,128)(2,1)} %add_convert_fusion.dn_p, bf16[704,2048]{1,0:T(8,128)(2,1)} %convolution_convert_fusion.3.feed_p, ...), custom_call_target="tpu_custom_call" | custom-call | tf_op jit(solution)/shard_map/back/pallas_call | solution.py:1233
  338.2 10.3 %finish.1 = (f32[176,2048]{1,0:T(8,128)}, f32[176,2048]{1,0:T(8,128)}, f32[1,128,2816]{2,1,0:T(8,128)}, f32[1,128,2816]{2,1,0:T(8,128)}, f32[1,2816,128]{2,1,0:T...) custom-call(f32[176,2048]{1,0:T(8,128)} %get-tuple-element.42.mid_h,, ...), custom_call_target="tpu_custom_call" | custom-call | tf_op jit(solution)/shard_map/finish/pallas_call | solution.py:1367
Async XLA Ops:
  149.6 5.3 %copy-start = (bf16[3,704,2048]{2,1,0:T(8,128)(2,1)S(1)}, bf16[3,704,2048]{2,1,0:T(8,128)(2,1)}, u32[]{:S(2)}) copy-start(bf16[3,704,2048]{2,1,0:T(8,128)(2,1)} %get-tuple-element.44) | copy-start | bytes 25952260
  149.6 6.0 %copy-start.2 = (bf16[704,2048]{1,0:T(8,128)(2,1)S(1)}, bf16[704,2048]{1,0:T(8,128)(2,1)}, u32[]{:S(2)}) copy-start(bf16[704,2048]{1,0:T(8,128)(2,1)} %get-tuple-element.43) | copy-start | bytes 8650756
  155.6 2.5 copy-start.1

commit v3 on v2

--- a/solution.py
+++ b/solution.py
@@ -334,6 +334,10 @@
     return pl.ds(pl.multiple_of(r * height, 16), height)
 
 
+def tokens(o, pitch, count):
+    return pl.ds(pl.multiple_of(o * pitch, 16), count)
+
+
 def greet(peers):
     barrier = pltpu.get_barrier_semaphore()
     for peer in peers:
@@ -392,7 +396,7 @@
 
 def params(cid):
     return pltpu.CompilerParams(
-        collective_id=cid, has_side_effects=True, vmem_limit_bytes=60 * 1024 * 1024
+        collective_id=cid, has_side_effects=True, vmem_limit_bytes=67043328
     )
 
 
@@ -426,6 +430,13 @@
         return carry
 
     lax.fori_loop(0, height // step, wrapped, 0)
+
+
+def add_into(dst, src, height, step):
+    def one(r):
+        dst[r, :] = (dst[r, :].astype(F32) + src[r, :].astype(F32)).astype(dst.dtype)
+
+    by_rows(height, step, one)
 
 
 def swap_halves(v):
@@ -449,6 +460,7 @@
     def __init__(self, wire, own, buf, send_base, recv_base):
         self.wire, self.own, self.buf = wire, own, buf
         self.s, self.r = send_base, recv_base
+        self.pitch = buf.shape[0] // ZN
         z, x, c, y = place()
         self.z, self.y = z, y
         self.up, self.down = dev(z + 1, x, c, y), dev(z - 1, x, c, y)
@@ -456,7 +468,7 @@
         self.seq, self.half = own.shape[0], own.shape[1] // 2
 
     def blk(self, o, h):
-        return self.buf.at[rows(o, self.seq), lanes(h, self.half)]
+        return self.buf.at[tokens(o, self.pitch, self.seq), lanes(h, self.half)]
 
     def start(self):
         z, wire = self.z, self.wire
@@ -476,9 +488,41 @@
             wire.send(b, b, self.s + base + o, self.r + o, to, cond & fwd)
             wire.send(b, b, self.s + 8 + o, self.r + 4 + o, self.other, cond)
 
-    def finish(self):
-        for o in range(ZN):
-            self.wire.arrived(self.blk(o, 1 - self.y), self.r + 4 + o, self.other, self.z != o)
+    def half_of(self, o):
+        self.wire.arrived(self.blk(o, 1 - self.y), self.r + 4 + o, self.other)
+
+
+class Chain:
+    def __init__(self, wire, held, zin, height, step, send_base, recv_base):
+        self.wire, self.held, self.zin = wire, held, zin
+        self.height, self.step = height, step
+        self.s, self.r = send_base, recv_base
+        self.z, x, c, y = place()
+        self.up, self.down = dev(self.z + 1, x, c, y), dev(self.z - 1, x, c, y)
+
+    def inbound(self, o, slot, frm, cond):
+        self.wire.arrived(self.zin(slot), self.r + slot, frm, cond)
+
+        @pl.when(cond)
+        def _():
+            add_into(self.held(o), self.zin(slot), self.height, self.step)
+
+    def outward(self, t, ready):
+        z = self.z
+        for o, cond, more, to, frm, base, slot in (
+            (z + t, z + t < ZN, z > 0, self.up, self.down, 0, z + t),
+            (z - t, z >= t, z < ZN - 1, self.down, self.up, 4, 4 if t == 1 else z - t),
+        ):
+            ready(o, cond)
+            self.inbound(o, o, frm, cond & more)
+            self.wire.send(
+                self.held(o), self.zin(slot), self.s + base + o, self.r + slot, to, cond
+            )
+
+    def home(self):
+        z = self.z
+        self.inbound(z, z, self.down, z > 0)
+        self.inbound(z, 4, self.up, z < ZN - 1)
 
 
 class Tree:
@@ -538,12 +582,15 @@
 
 def front_kernel(
     resid_h, wq_l, wk_l, wv_l, wo_l, g1_l, g2_l, wg_h, wu_h, wd_h, cot_h, seg, freq,
-    wqkv, wo, ga, w3, dres, n1, q, kv, ctx, mid, normed, cos_t, sin_t, mask,
+    wqkv_o, wo_o, ga, n1_o, q_o, kv, ctx_o, mid_o, cos_t, sin_t, mask, dn, feed_out, g3_out,
+    wqkv, wo, n1, q, ctx, mid, zin, w3, dres, normed, hid_t, dg_t, du_t, hid, dg, du, dnp, yin, stage,
     resid, wg_l, wu_l, cot, ga_l, qkv_l, w3_l, dres_l, kx, vx, attn, part, nrm, ss, rs, ls,
 ):
     z, x, c, y = place()
     units = w3.shape[1]
     seq, width = resid.shape
+    half = width // 2
+    pitch = normed.shape[0] // ZN
     q_width = q.shape[1]
     pairs = q_width // LANE
     loads = [
@@ -638,6 +685,10 @@
     lane = lax.broadcasted_iota(jnp.int32, (seq, LANE), 1)
     cos_t[...] = jnp.cos(angles)
     sin_t[...] = jnp.where(lane % HD < HD // 2, -1.0, 1.0) * jnp.sin(angles)
+    for o in range(ZN):
+        gap = pl.ds(o * pitch + seq, pitch - seq)
+        normed[gap, :] = jnp.zeros((pitch - seq, width), BF)
+        dres[gap, :] = jnp.zeros((pitch - seq, width), BF)
     loads[0].wait()
     by_rows(seq, 16, round_cot)
     t_ga.relay(1)
@@ -671,10 +722,10 @@
     t_wo.relay(1)
     t_qkv.across(2)
     t_wo.relay(2)
-    l_dres.start()
     for d in (2, 1, 3):
         zt = (z + d) % ZN
         wire.send(w3_l.at[:, rows(zt, units), :], ffn(mine), 60 + d - 1, 48 + z, dev(zt, x, c, y))
+    l_dres.start()
     t_qkv.across(3)
     t_qkv.finish()
     own[0].wait()
@@ -693,7 +744,7 @@
     wire.send(mine3, ffn(mine), 68 + z * 2 + x, 56 + z * 2 + x, twin)
     own += [
         pltpu.make_async_copy(mine3, ffn(mine), ls.at[3]),
-        pltpu.make_async_copy(dres_l, dres.at[rows(z, seq), :], ls.at[4]),
+        pltpu.make_async_copy(dres_l, dres.at[tokens(z, pitch, seq), :], ls.at[4]),
     ]
     own[3].start()
     own[4].start()
@@ -710,6 +761,14 @@
 
     lax.fori_loop(0, width // (2 * LANE), out_tile, 0)
     wire.send(attn, part, 100, 80, other)
+    kept = [
+        pltpu.make_async_copy(a, b, ls.at[17 + i])
+        for i, (a, b) in enumerate(
+            ((wqkv, wqkv_o), (wo, wo_o), (n1, n1_o), (q, q_o), (ctx, ctx_o), (mid, mid_o))
+        )
+    ]
+    for cp in kept[:5]:
+        cp.start()
 
     def ffn_in(d):
         o = (z + ZN - d) % ZN
@@ -731,30 +790,134 @@
         recip = lax.rsqrt(jnp.mean(m * m, axis=-1, keepdims=True) + epsilon)
         nrm[r, :] = (m * recip * gain_two).astype(BF)
 
-    l_dres.relay(1)
     ffn_in(2)
     wire.arrived(part, 80, other)
     by_rows(seq, 16, second)
     l_norm.start()
-    own.append(pltpu.make_async_copy(nrm, normed.at[rows(z, seq), :], ls.at[5]))
+    kept[5].start()
+    own.append(pltpu.make_async_copy(nrm, normed.at[tokens(z, pitch, seq), :], ls.at[5]))
     own[5].start()
-    l_dres.relay(2)
     ffn_in(1)
     ffn_across(0)
+    ffn_in(3)
+    l_dres.relay(1)
+    ffn_across(2)
     l_norm.relay(1)
-    ffn_in(3)
-    l_dres.relay(3)
-    l_norm.relay(2)
-    l_norm.relay(3)
-    for d in (2, 1, 3):
-        ffn_across(d)
+    l_dres.relay(2)
+    ffn_across(1)
+    ffn_across(3)
     for o in range(ZN):
         for xx in (0, 1):
             wire.arrived(ffn(rid(o, xx, 1 - c)), 56 + o * 2 + xx, twin)
-    l_dres.finish()
-    l_norm.finish()
+    for cp in own[3:]:
+        cp.wait()
+    step = units // 2
+
+    def ffn_block(o):
+        r = tokens(o, pitch, pitch)
+
+        def some_units(i, carry):
+            u = pl.ds(pl.multiple_of(i * step, 16), step)
+            g = dot_nt(w3[0, u, :], normed[r, :])
+            up = dot_nt(w3[1, u, :], normed[r, :])
+            dh = dot_nt(w3[2, u, :], dres[r, :])
+            s = jax.nn.sigmoid(g)
+            hid_t[u, lanes(o, pitch)] = (g * s * up).astype(BF)
+            dg_t[u, lanes(o, pitch)] = (dh * up * s * (1.0 + g * (1.0 - s))).astype(BF)
+            du_t[u, lanes(o, pitch)] = (dh * (g * s)).astype(BF)
+            return carry
+
+        lax.fori_loop(0, units // step, some_units, 0)
+        dg[...] = dg_t[:, lanes(o, pitch)].astype(F32).T[:seq].astype(BF)
+        du[...] = du_t[:, lanes(o, pitch)].astype(F32).T[:seq].astype(BF)
+        hid[rows(o, seq), :] = hid_t[:, lanes(o, pitch)].astype(F32).T[:seq].astype(BF)
+
+        def some_lanes(j, carry):
+            cut = lanes(j, 2 * LANE)
+            dnp[o, :, cut] = (dot_nn(dg[...], w3[0, :, cut]) + dot_nn(du[...], w3[1, :, cut])).astype(BF)
+            return carry
+
+        lax.fori_loop(0, width // (2 * LANE), some_lanes, 0)
+
+    def far_half(o):
+        part = dnp.at[o].at[:, lanes(1 - y, half)]
+        wire.send(part, yin.at[o], 101 + o, 81 + o, other)
+
+    o1 = z + 1 - 2 * ((z + 3) // 4)
+    o3 = 3 - 3 * (z // 2)
+    o2 = 6 - z - o1 - o3
+
+    def both_halves(o):
+        l_dres.half_of(o)
+        l_norm.half_of(o)
+
+    ffn_block(z)
+    l_norm.relay(2)
+    l_dres.relay(3)
+    both_halves(o1)
+    ffn_block(o1)
+    l_norm.relay(3)
+    both_halves(o2)
+    ffn_block(o2)
+    far_half(o2)
+    both_halves(o3)
+    ffn_block(o3)
+    for o in (o3, o1, z):
+        far_half(o)
+
+    wide = 4 * LANE
+    tiles = width // wide
+
+    def columns(first, value, dst):
+        def one(j, carry):
+            slot = j % 2
+            cp = pltpu.make_async_copy(stage.at[slot], dst(j), ls.at[11 + slot])
+            if first:
+                pl.when(j >= 2)(cp.wait)
+            else:
+                cp.wait()
+            stage[slot] = value(lanes(j, wide)).astype(BF)
+            cp.start()
+            return carry
+
+        lax.fori_loop(0, tiles, one, 0)
+
+    def over_tokens(act, kept):
+        return lambda cut: dot_nn(act[...], kept[:, cut])
+
+    def grad_dst(m):
+        return lambda j: g3_out.at[m, :, lanes(j, wide)]
+
+    line = Chain(wire, lambda o: yin.at[o], lambda k: zin.at[k], seq, 16, 105, 85)
+
+    def dn_ready(o, cond):
+        wire.arrived(yin.at[o], 81 + o, other, cond)
+
+        @pl.when(cond)
+        def _():
+            add_into(yin.at[o], dnp.at[o].at[:, lanes(y, half)], seq, 16)
+
+    columns(True, over_tokens(dg_t, normed), grad_dst(0))
+    line.outward(3, dn_ready)
+    columns(False, over_tokens(du_t, normed), grad_dst(1))
+    line.outward(2, dn_ready)
+    columns(False, over_tokens(hid_t, dres), grad_dst(2))
+    line.outward(1, dn_ready)
+    columns(False, lambda cut: dot_nn(hid[...], w3[2, :, cut]), lambda j: feed_out.at[:, lanes(j, wide)])
+    dn_ready(z, z >= 0)
+    line.home()
+
+    def keep_dn(r):
+        dn[r, lanes(y, half)] = yin[z, r, :]
+
+    by_rows(seq, 16, keep_dn)
+    blk = dn.at[:, lanes(y, half)]
+    wire.send(blk, blk, 113, 90, other)
+    wire.arrived(dn.at[:, lanes(1 - y, half)], 90, other)
     wire.drain()
-    for cp in own[3:]:
+    for slot in (0, 1):
+        pltpu.make_async_copy(stage.at[slot], feed_out.at[:, lanes(slot, wide)], ls.at[11 + slot]).wait()
+    for cp in kept:
         cp.wait()
 
 
@@ -764,6 +927,7 @@
     total = q_width + 2 * LANE
     units = w_gate.shape[2] // ZN
     pair_shape = (4, seq, LANE)
+    pitch = pl.cdiv(seq, LANE) * LANE
     freq = rope_base ** (-(np.arange(LANE) % (HD // 2)) * 2.0 / HD)
     freq = jnp.asarray(freq[None].astype(np.float32))
     vm, hb = vm_spec(), any_spec()
@@ -774,21 +938,40 @@
             jax.ShapeDtypeStruct((width, total), BF),
             jax.ShapeDtypeStruct((out_rows, width), BF),
             jax.ShapeDtypeStruct((16, width), BF),
-            jax.ShapeDtypeStruct((3, units, width), BF),
-            jax.ShapeDtypeStruct((seq * ZN, width), BF),
             jax.ShapeDtypeStruct((seq, width), BF),
             jax.ShapeDtypeStruct((seq, q_width), BF),
             jax.ShapeDtypeStruct((seq, 2 * LANE), BF),
             jax.ShapeDtypeStruct((seq, q_width), BF),
             jax.ShapeDtypeStruct((seq, width), F32),
-            jax.ShapeDtypeStruct((seq * ZN, width), BF),
             jax.ShapeDtypeStruct((seq, LANE), F32),
             jax.ShapeDtypeStruct((seq, LANE), F32),
             jax.ShapeDtypeStruct((seq, seq), F32),
+            jax.ShapeDtypeStruct((seq, width), BF),
+            jax.ShapeDtypeStruct((seq * ZN, width), BF),
+            jax.ShapeDtypeStruct((3, units, width), BF),
         ),
         in_specs=[hb] + [vm] * 6 + [hb] * 4 + [vm] * 2,
-        out_specs=[vm] * 3 + [hb] * 2 + [vm] * 5 + [hb] + [vm] * 3,
+        out_specs=[hb] * 2 + [vm] + [hb] * 2 + [vm] + [hb] * 2 + [vm] * 4 + [hb] * 2,
         scratch_shapes=[
+            pltpu.VMEM((width, total), BF),
+            pltpu.VMEM((out_rows, width), BF),
+            pltpu.VMEM((seq, width), BF),
+            pltpu.VMEM((seq, q_width), BF),
+            pltpu.VMEM((seq, q_width), BF),
+            pltpu.VMEM((seq, width), F32),
+            pltpu.VMEM((5, seq, width // 2), BF),
+            pltpu.VMEM((3, units, width), BF),
+            pltpu.VMEM((pitch * ZN, width), BF),
+            pltpu.VMEM((pitch * ZN, width), BF),
+            pltpu.VMEM((units, pitch * ZN), BF),
+            pltpu.VMEM((units, pitch * ZN), BF),
+            pltpu.VMEM((units, pitch * ZN), BF),
+            pltpu.VMEM((seq * ZN, units), BF),
+            pltpu.VMEM((seq, units), BF),
+            pltpu.VMEM((seq, units), BF),
+            pltpu.VMEM((ZN, seq, width), BF),
+            pltpu.VMEM((ZN, seq, width // 2), BF),
+            pltpu.VMEM((2, seq * ZN, 4 * LANE), BF),
             pltpu.VMEM((seq, width), F32),
             pltpu.VMEM((LANE, units * ZN), BF),
             pltpu.VMEM((LANE, units * ZN), BF),
@@ -802,52 +985,12 @@
             pltpu.VMEM((seq, width), BF),
             pltpu.VMEM((seq, width), BF),
             pltpu.VMEM((seq, width), BF),
-            sems(101),
-            sems(81),
-            sems(11),
+            sems(114),
+            sems(91),
+            sems(23),
         ],
         compiler_params=params(0),
     )(resid, w_query, w_key, w_value, w_out, g1, g2, w_gate, w_up, w_down, cot, seg, freq)
-
-
-def add_into(dst, src, height, step):
-    def one(r):
-        dst[r, :] = (dst[r, :].astype(F32) + src[r, :].astype(F32)).astype(dst.dtype)
-
-    by_rows(height, step, one)
-
-
-class Chain:
-    def __init__(self, wire, held, zin, height, step, send_base, recv_base):
-        self.wire, self.held, self.zin = wire, held, zin
-        self.height, self.step = height, step
-        self.s, self.r = send_base, recv_base
-        self.z, x, c, y = place()
-        self.up, self.down = dev(self.z + 1, x, c, y), dev(self.z - 1, x, c, y)
-
-    def inbound(self, o, slot, frm, cond):
-        self.wire.arrived(self.zin(slot), self.r + slot, frm, cond)
-
-        @pl.when(cond)
-        def _():
-            add_into(self.held(o), self.zin(slot), self.height, self.step)
-
-    def outward(self, t, ready):
-        z = self.z
-        for o, cond, more, to, frm, base, slot in (
-            (z + t, z + t < ZN, z > 0, self.up, self.down, 0, z + t),
-            (z - t, z >= t, z < ZN - 1, self.down, self.up, 4, 4 if t == 1 else z - t),
-        ):
-            ready(o, cond)
-            self.inbound(o, o, frm, cond & more)
-            self.wire.send(
-                self.held(o), self.zin(slot), self.s + base + o, self.r + slot, to, cond
-            )
-
-    def home(self):
-        z = self.z
-        self.inbound(z, z, self.down, z > 0)
-        self.inbound(z, 4, self.up, z < ZN - 1)
 
 
 class Fold:
@@ -922,11 +1065,11 @@
 
 
 def back_kernel(
-    dn_p, feed_p, g3_p, wqkv, mid_h, cot_h, resid_h, ga_h, n1_h, q_h, kv_h, ctx_h, wo_h, cos_h,
+    feed_p, g3_p, wqkv, dn_h, mid_h, cot_h, resid_h, ga_h, n1_h, q_h, kv_h, ctx_h, wo_h, cos_h,
     sin_h, mask_h,
     feed_out, grad_out, g3, gq_out, go_out, gains_out,
-    mid, cot, resid, ga, n1, q, kv, ctx, wo, cos_t, sin_t, mask, grad_in, fown, yin, zin, gbuf, cin, xin, gq_p, go_p, gp, qc, qx, qz, oc, ox, oz, gc, gx, gz,
-    dn, feed, mid_b, dctx, dqkv, dn1, dn1_o, kx, vx, kacc, vacc, wbuf, gs, gr, ss, rs, ls,
+    dn, mid, cot, resid, ga, n1, q, kv, ctx, wo, cos_t, sin_t, mask, grad_in, fown, yin, zin, gbuf, cin, xin, gq_p, go_p, gp, qc, qx, qz, oc, ox, oz, gc, gx, gz,
+    feed, mid_b, dctx, dqkv, dn1, dn1_o, kx, vx, kacc, vacc, wbuf, gs, gr, ss, rs, ls,
 ):
     z, x, c, y = place()
     units = g3_p.shape[1]
@@ -940,24 +1083,18 @@
     ring = [(z + d) % ZN for d in (2, 1, 3, 0)]
     greet(all_peers(z, x, c, y))
 
-    def y_out(src, k):
-        for t in (3, 2, 1):
-            for o, cond in ((z + t, z + t < ZN), (z - t, z >= t)):
-                s = src.at[rows(o, seq), lanes(1 - y, half)]
-                wire.send(s, yin.at[k, o], k * 4 + o, k * 4 + o, other, cond)
-        s = src.at[rows(z, seq), lanes(1 - y, half)]
-        wire.send(s, yin.at[k, z], k * 4 + z, k * 4 + z, other)
-
-    y_out(dn_p, 0)
-
-    def own_half(k, o):
-        src = (dn_p, feed_p)[k]
+    def y_out(src, k, steps):
+        for t in steps:
+            todo = ((z + t, z + t < ZN), (z - t, z >= t)) if t else ((z, None),)
+            for o, cond in todo:
+                part = src.at[rows(o, seq), lanes(1 - y, half)]
+                wire.send(part, yin.at[o], k * 4 + o, k * 4 + o, other, cond)
+
+    def own_half(o):
         return pltpu.make_async_copy(
-            src.at[rows(o, seq), lanes(y, half)], fown.at[k, o], ls.at[2 + k * 4 + o]
+            feed_p.at[rows(o, seq), lanes(y, half)], fown.at[o], ls.at[3 + o]
         )
 
-    for o in range(ZN):
-        own_half(0, o).start()
     for k in range(8):
         wire.send(g3_p.at[:, :, lanes(k * 2 + 1 - c)], cin.at[k], 26 + k, 20 + k, twin)
     ks = [o * 2 + 1 - x for o in ring] + [o * 2 + x for o in ring]
@@ -971,8 +1108,8 @@
         for m in range(3):
             add_into(dst.at[m], src.at[m], units, 64)
 
-    load(0).start()
-    for i in range(8):
+
+    def ffn_add(i):
         if i < 7:
             load(i + 1).start()
         load(i).wait()
@@ -981,8 +1118,10 @@
         if i < 4:
             o = ring[i]
             wire.send(cin.at[ks[i]], xin.at[o], 34 + o, 28 + o, side)
+
+    load(0).start()
     pairs_in = (
-        (wo_h, wo), (ga_h, ga), (kv_h, kv), (mask_h, mask), (mid_h, mid), (cot_h, cot), (n1_h, n1),
+        (dn_h, dn), (mid_h, mid), (cot_h, cot), (wo_h, wo), (ga_h, ga), (kv_h, kv), (mask_h, mask), (n1_h, n1),
         (q_h, q), (ctx_h, ctx), (cos_h, cos_t), (sin_h, sin_t), (resid_h, resid),
     )
     inward = [
@@ -991,33 +1130,9 @@
     for cp in inward:
         cp.start()
     for o in range(ZN):
-        own_half(1, o).start()
-        own_half(0, o).wait()
-    def chain_of(k):
-        return Chain(
-            wire, lambda o: yin.at[k, o], lambda s: zin.at[k, s], seq, 16, 8 + k * 8, 8 + k * 5
-        )
-
-    def dn_ready(o, cond):
-        wire.arrived(yin.at[0, o], o, other, cond)
-
-        @pl.when(cond)
-        def _():
-            add_into(yin.at[0, o], fown.at[0, o], seq, 16)
-
-    line = chain_of(0)
-    for t in (3, 2, 1):
-        line.outward(t, dn_ready)
-    dn_ready(z, z >= 0)
-    line.home()
-    blk = dn.at[:, lanes(y, half)]
-
-    def keep_dn(r):
-        dn[r, lanes(y, half)] = yin[0, z, r, :]
-
-    by_rows(seq, 16, keep_dn)
-    wire.send(blk, blk, 24, 18, other)
-    y_out(feed_p, 1)
+        own_half(o).start()
+
+    line = Chain(wire, lambda o: yin.at[o], lambda k: zin.at[k], seq, 16, 8, 8)
 
     def ffn_z(i):
         o = ring[i]
@@ -1029,8 +1144,9 @@
         else:
             pltpu.make_async_copy(xin.at[o], g3.at[:, rows(z, units), :], ls.at[10]).start()
 
-    ffn_z(0)
-    ffn_z(1)
+    y_out(feed_p, 1, (3, 2, 1, 0))
+    for i in range(8):
+        ffn_add(i)
     for cp in inward:
         cp.wait()
     spread_pair(kx, kv[:, pl.ds(0, LANE)].astype(F32))
@@ -1040,7 +1156,6 @@
     gp[...] = jnp.zeros_like(gp)
     gain_one = ga[pl.ds(0, 8), :].astype(F32)[0:1]
     gain_two = ga[pl.ds(0, 8), :].astype(F32)[1:2]
-    wire.arrived(dn.at[:, lanes(1 - y, half)], 18, other)
 
     def norm_two(r):
         v, g = mid[r, :], dn[r, :].astype(F32)
@@ -1078,8 +1193,7 @@
         return carry
 
     lax.fori_loop(0, q_width // (2 * LANE), ctx_grad, 0)
-    ffn_z(2)
-    ffn_z(3)
+    ffn_z(0)
     f_o.across()
 
     def back_turned(v):
@@ -1106,7 +1220,9 @@
         dqkv[:, lanes(p)] = back_turned(dq * HD ** (-0.5)).astype(BF)
         return carry
 
-    lax.fori_loop(0, pairs, pair, 0)
+    lax.fori_loop(0, pairs // 2, pair, 0)
+    ffn_z(1)
+    lax.fori_loop(pairs // 2, pairs, pair, 0)
 
     def joined(acc):
         low = lax.broadcasted_iota(jnp.int32, (seq, LANE), 1) < HD
@@ -1132,6 +1248,7 @@
     lax.fori_loop(0, width // LANE, in_grad, 0)
     f_q.to_twin()
     f_q.across()
+    ffn_z(2)
     tiles = width // (2 * LANE)
     for j in range(tiles):
         if j + 1 < tiles:
@@ -1149,21 +1266,21 @@
     by_rows(seq, 16, gain_part)
     f_g.to_twin()
     f_g.across()
+    ffn_z(3)
     f_o.stay()
     for t in (3, 2, 1):
         f_o.outward(t)
 
     for o in range(ZN):
-        own_half(1, o).wait()
+        own_half(o).wait()
 
     def feed_ready(o, cond):
-        wire.arrived(yin.at[1, o], 4 + o, other, cond)
+        wire.arrived(yin.at[o], 4 + o, other, cond)
 
         @pl.when(cond)
         def _():
-            add_into(yin.at[1, o], fown.at[1, o], seq, 16)
-
-    line = chain_of(1)
+            add_into(yin.at[o], fown.at[o], seq, 16)
+
     for t in (3, 2, 1):
         line.outward(t, feed_ready)
     f_q.stay()
@@ -1176,7 +1293,7 @@
     fb = feed.at[:, lanes(y, half)]
 
     def keep_feed(r):
-        feed[r, lanes(y, half)] = yin[1, z, r, :]
+        feed[r, lanes(y, half)] = yin[z, r, :]
 
     by_rows(seq, 16, keep_feed)
     wire.send(fb, fb, 25, 19, other)
@@ -1191,19 +1308,19 @@
         grad_in[r, :] += d
 
     by_rows(seq, 16, norm_one)
-    outward = [pltpu.make_async_copy(grad_in, grad_out, ls.at[25])]
+    outward = [pltpu.make_async_copy(grad_in, grad_out, ls.at[26])]
     outward[0].start()
     done = f_o.home()
-    outward.append(pltpu.make_async_copy(done, go_out, ls.at[26]))
+    outward.append(pltpu.make_async_copy(done, go_out, ls.at[27]))
     outward[1].start()
     mine = f_g.home()
     gs[...] = mine[...]
     wire.send(gs, gr, 102, 88, other)
     got = f_q.home()
-    outward.append(pltpu.make_async_copy(got, gq_out, ls.at[27]))
+    outward.append(pltpu.make_async_copy(got, gq_out, ls.at[28]))
     outward[2].start()
     wire.arrived(feed.at[:, lanes(1 - y, half)], 19, other)
-    outward.append(pltpu.make_async_copy(feed, feed_out, ls.at[28]))
+    outward.append(pltpu.make_async_copy(feed, feed_out, ls.at[29]))
     outward[3].start()
     wire.arrived(gr, 88, other)
     first = jnp.sum(gs[pl.ds(0, 8), :] + gr[pl.ds(0, 8), :], axis=0, keepdims=True)
@@ -1219,7 +1336,7 @@
         cp.wait()
 
 
-def back(dn_p, feed_p, g3_p, wqkv, mid, cot, resid, ga, n1, q, kv, ctx, wo, cos_t, sin_t, mask):
+def back(feed_p, g3_p, wqkv, dn, mid, cot, resid, ga, n1, q, kv, ctx, wo, cos_t, sin_t, mask):
     seq, width = mid.shape
     units = g3_p.shape[1]
     q_width, total = q.shape[1], wqkv.shape[1]
@@ -1229,7 +1346,7 @@
     def vm(*shape, dtype=BF):
         return pltpu.VMEM(shape, dtype)
 
-    held = (mid, cot, resid, ga, n1, q, kv, ctx, wo, cos_t, sin_t, mask)
+    held = (dn, mid, cot, resid, ga, n1, q, kv, ctx, wo, cos_t, sin_t, mask)
     return pl.pallas_call(
         back_kernel,
         name="back",
@@ -1246,9 +1363,9 @@
         scratch_shapes=[vm(*a.shape, dtype=a.dtype) for a in held]
         + [
             vm(seq, width, dtype=F32),
-            vm(2, ZN, seq, half),
-            vm(2, ZN, seq, half),
-            vm(2, 5, seq, half),
+            vm(ZN, seq, half),
+            vm(ZN, seq, half),
+            vm(5, seq, half),
             vm(2, 3, units, LANE),
             vm(8, 3, units, LANE),
             vm(4, 3, units, LANE),
@@ -1266,7 +1383,6 @@
             vm(5, 16, LANE, dtype=F32),
             vm(seq, width),
             vm(seq, width),
-            vm(seq, width),
             vm(seq, q_width),
             vm(seq, total),
             vm(seq, width),
@@ -1280,12 +1396,12 @@
             vm(16, LANE, dtype=F32),
             sems(103),
             sems(89),
-            sems(29),
+            sems(30),
         ],
         compiler_params=pltpu.CompilerParams(
             collective_id=1, has_side_effects=True, vmem_limit_bytes=67043328
         ),
-    )(dn_p, feed_p, g3_p, wqkv, *held)
+    )(feed_p, g3_p, wqkv, *held)
 
 
 def finish_kernel(
@@ -1409,31 +1525,12 @@
     cotangent,
 ):
     resid = hidden_in
-    wqkv, wo, ga, w3, dres_all, n1, q, kv, ctx, middle, normed_all, cos_w, sin_w, mask = front(
+    wqkv, wo, ga, n1, q, kv, ctx, middle, cos_w, sin_w, mask, dn, feed_p, g3_p = front(
         resid, w_query, w_key, w_value, w_out, gain_attn, gain_ffn, w_gate, w_up, w_down,
         cotangent, segment_ids,
     )
-    gate = contract_cols(normed_all, w3[0])
-    up_proj = contract_cols(normed_all, w3[1])
-    sigma = jax.nn.sigmoid(gate)
-    hidden_act = (gate * sigma * up_proj).astype(BF)
-    grad_hidden = contract_cols(dres_all, w3[2])
-    grad_gate_b = (grad_hidden * up_proj * sigma * (1.0 + gate * (1.0 - sigma))).astype(BF)
-    grad_up_b = (grad_hidden * (gate * sigma)).astype(BF)
-    feed_p = jnp.dot(hidden_act, w3[2], preferred_element_type=F32).astype(BF)
-    dn_p = (
-        jnp.dot(grad_gate_b, w3[0], preferred_element_type=F32)
-        + jnp.dot(grad_up_b, w3[1], preferred_element_type=F32)
-    ).astype(BF)
-    g3_p = jnp.stack(
-        [
-            contract_rows(grad_gate_b, normed_all).astype(BF),
-            contract_rows(grad_up_b, normed_all).astype(BF),
-            contract_rows(hidden_act, dres_all).astype(BF),
-        ]
-    )
     feed, grad_b, g3, gq, go, gains_g = back(
-        dn_p, feed_p, g3_p, wqkv, middle, cotangent, resid, ga, n1, q, kv, ctx, wo,
+        feed_p, g3_p, wqkv, dn, middle, cotangent, resid, ga, n1, q, kv, ctx, wo,
         cos_w, sin_w, mask,
     )
     hidden_out, grad_input, wg, wu, wd, wq, wk, wv, wo_g, first, second = finish(

time: 349 us -> 339 us (0.971)
  matrix products: 28.9 us -> 0 us
  Pallas kernels: 314 us -> 337 us
  other arithmetic: 3.95 us -> 0 us
    pallas_call x1, Pallas kernels: 149 us -> 199 us  [front(): pl.pallas_call(front_kernel, name='front', out_shape=(jax.ShapeDtypeStruc...]
    dot_general x9 -> x0, matrix products: 28.9 us -> none  [the longest x3 10.9 us: contract_cols(): lax.dot_general(left, right, (((1,), (1,)), ((), ())), preferred_element_...]
    pallas_call x1, Pallas kernels: 155 us -> 128 us  [back(): pl.pallas_call(back_kernel, name='back', out_shape=(jax.ShapeDtypeStruct(...]
    another operation x1 -> x0, other arithmetic: 3.95 us -> none  [fast_body(): jnp.stack([contract_rows(grad_gate_b, normed_all).astype(BF), contract_ro...]
where the time goes in v3:
time: 339 us; the launch traced here: 338 us
  Pallas kernels  337 us (99%)
    pallas_call x1, Pallas kernels, front(): pl.pallas_call(front_kernel, name='front', out_shape=(jax.ShapeDtypeStruc...  199 us
    pallas_call x1, Pallas kernels, back(): pl.pallas_call(back_kernel, name='back', out_shape=(jax.ShapeDtypeStruct(...  128 us
    pallas_call x1, Pallas kernels, finish(): pl.pallas_call(finish_kernel, name='finish', out_shape=(f32(seq, width),...  10.3 us

profile of v3, /device:TPU:0, one launch (start us, length us, event | category | flops | bytes accessed | tf_op | source)
XLA Modules:
  0.0 337.5 jit_solution(9476024924659290469)
XLA Ops:
  0.6 198.5 %front.1 = (bf16[2048,1280]{1,0:T(8,128)(2,1)}, bf16[1024,2048]{1,0:T(8,128)(2,1)}, bf16[16,2048]{1,0:T(8,128)(2,1)}, bf16[176,2048]{1,0:T(8,128)(2,1)}, bf16[17...) custom-call(f32[176,2048]{1,0:T(8,128)} %resid_h.3, ...), custom_call_target="tpu_custom_call" | custom-call | tf_op jit(solution)/shard_map/front/pallas_call | solution.py:934
  199.2 127.9 %back.1 = (bf16[176,2048]{1,0:T(8,128)(2,1)}, f32[176,2048]{1,0:T(8,128)}, bf16[3,2816,128]{2,1,0:T(8,128)(2,1)}, bf16[128,1280]{1,0:T(8,128)(2,1)}, bf16[1024,128]{1,0:T(8,128)(2,1)}, /*index=5*/f32[8,128]{1,0:T(8,128)}) custom-call(bf16[704,2048]{1,0:T(8,128)(2,1)} %get-tuple-element.43.feed_p, bf16[3,704,2048]{2,1,0:T(8,128)(2,1)} %get-tuple-element.44.g3_p, ...), custom_call_target="tpu_custom_call" | custom-call | tf_op jit(solution)/shard_map/back/pallas_call | solution.py:1350
  327.1 10.3 %finish.1 = (f32[176,2048]{1,0:T(8,128)}, f32[176,2048]{1,0:T(8,128)}, f32[1,128,2816]{2,1,0:T(8,128)}, f32[1,128,2816]{2,1,0:T(8,128)}, f32[1,2816,128]{2,1,0:T...) custom-call(f32[176,2048]{1,0:T(8,128)} %get-tuple-element.42.mid_h,, ...), custom_call_target="tpu_custom_call" | custom-call | tf_op jit(solution)/shard_map/finish/pallas_call | solution.py:1483

commit v4 on v3

--- a/solution.py
+++ b/solution.py
@@ -888,7 +888,23 @@
     def grad_dst(m):
         return lambda j: g3_out.at[m, :, lanes(j, wide)]
 
-    line = Chain(wire, lambda o: yin.at[o], lambda k: zin.at[k], seq, 16, 105, 85)
+    quarter = half // 2
+
+    def part_chain(h):
+        cut = pl.ds(h * quarter, quarter)
+        return Chain(
+            wire,
+            lambda o: yin.at[o].at[:, cut],
+            lambda k: zin.at[k].at[:, cut],
+            seq, 16, 105 + 8 * h, 85 + 5 * h,
+        )
+
+    lines = [part_chain(0), part_chain(1)]
+
+    def outward(t):
+        lines[0].outward(t, dn_ready)
+        lines[1].outward(t, lambda o, cond: None)
+
 
     def dn_ready(o, cond):
         wire.arrived(yin.at[o], 81 + o, other, cond)
@@ -898,27 +914,24 @@
             add_into(yin.at[o], dnp.at[o].at[:, lanes(y, half)], seq, 16)
 
     columns(True, over_tokens(dg_t, normed), grad_dst(0))
-    line.outward(3, dn_ready)
+    outward(3)
     columns(False, over_tokens(du_t, normed), grad_dst(1))
-    line.outward(2, dn_ready)
+    outward(2)
     columns(False, over_tokens(hid_t, dres), grad_dst(2))
-    line.outward(1, dn_ready)
+    outward(1)
     columns(False, lambda cut: dot_nn(hid[...], w3[2, :, cut]), lambda j: feed_out.at[:, lanes(j, wide)])
     dn_ready(z, z >= 0)
-    line.home()
-
-    def keep_dn(r):
-        dn[r, lanes(y, half)] = yin[z, r, :]
-
-    by_rows(seq, 16, keep_dn)
-    blk = dn.at[:, lanes(y, half)]
-    wire.send(blk, blk, 113, 90, other)
-    wire.arrived(dn.at[:, lanes(1 - y, half)], 90, other)
+    for line in lines:
+        line.home()
+
+    keep_dn = pltpu.make_async_copy(yin.at[z], dn, ls.at[13])
+    keep_dn.start()
     wire.drain()
     for slot in (0, 1):
         pltpu.make_async_copy(stage.at[slot], feed_out.at[:, lanes(slot, wide)], ls.at[11 + slot]).wait()
     for cp in kept:
         cp.wait()
+    keep_dn.wait()
 
 
 def front(resid, w_query, w_key, w_value, w_out, g1, g2, w_gate, w_up, w_down, cot, seg):
@@ -946,12 +959,12 @@
             jax.ShapeDtypeStruct((seq, LANE), F32),
             jax.ShapeDtypeStruct((seq, LANE), F32),
             jax.ShapeDtypeStruct((seq, seq), F32),
-            jax.ShapeDtypeStruct((seq, width), BF),
+            jax.ShapeDtypeStruct((seq, width // 2), BF),
             jax.ShapeDtypeStruct((seq * ZN, width), BF),
             jax.ShapeDtypeStruct((3, units, width), BF),
         ),
         in_specs=[hb] + [vm] * 6 + [hb] * 4 + [vm] * 2,
-        out_specs=[hb] * 2 + [vm] + [hb] * 2 + [vm] + [hb] * 2 + [vm] * 4 + [hb] * 2,
+        out_specs=[hb] * 2 + [vm] + [hb] * 2 + [vm] + [hb] * 2 + [vm] * 3 + [hb] * 3,
         scratch_shapes=[
             pltpu.VMEM((width, total), BF),
             pltpu.VMEM((out_rows, width), BF),
@@ -985,8 +998,8 @@
             pltpu.VMEM((seq, width), BF),
             pltpu.VMEM((seq, width), BF),
             pltpu.VMEM((seq, width), BF),
-            sems(114),
-            sems(91),
+            sems(121),
+            sems(95),
             sems(23),
         ],
         compiler_params=params(0),
@@ -1095,6 +1108,7 @@
             feed_p.at[rows(o, seq), lanes(y, half)], fown.at[o], ls.at[3 + o]
         )
 
+    wire.send(dn_h, dn.at[:, lanes(y, half)], 24, 18, other)
     for k in range(8):
         wire.send(g3_p.at[:, :, lanes(k * 2 + 1 - c)], cin.at[k], 26 + k, 20 + k, twin)
     ks = [o * 2 + 1 - x for o in ring] + [o * 2 + x for o in ring]
@@ -1121,7 +1135,7 @@
 
     load(0).start()
     pairs_in = (
-        (dn_h, dn), (mid_h, mid), (cot_h, cot), (wo_h, wo), (ga_h, ga), (kv_h, kv), (mask_h, mask), (n1_h, n1),
+        (dn_h, dn.at[:, lanes(y, half)]), (mid_h, mid), (cot_h, cot), (wo_h, wo), (ga_h, ga), (kv_h, kv), (mask_h, mask), (n1_h, n1),
         (q_h, q), (ctx_h, ctx), (cos_h, cos_t), (sin_h, sin_t), (resid_h, resid),
     )
     inward = [
@@ -1168,6 +1182,7 @@
         t = g * v * recip
         gp[pl.ds(8, 8), :] += t[:8] + t[8:]
 
+    wire.arrived(dn.at[:, lanes(1 - y, half)], 18, other)
     by_rows(seq, 16, norm_two)
 
     def out_grad(i, carry):
@@ -1360,7 +1375,8 @@
         ),
         in_specs=[any_spec()] * 16,
         out_specs=[any_spec()] * 5 + [vm_spec()],
-        scratch_shapes=[vm(*a.shape, dtype=a.dtype) for a in held]
+        scratch_shapes=[vm(seq, width)]
+        + [vm(*a.shape, dtype=a.dtype) for a in held[1:]]
         + [
             vm(seq, width, dtype=F32),
             vm(ZN, seq, half),

time: 339 us -> 332 us (0.979)
  Pallas kernels: 337 us -> 330 us
    pallas_call x1, Pallas kernels: 199 us -> 190 us  [front(): pl.pallas_call(front_kernel, name='front', out_shape=(jax.ShapeDtypeStruc...]
where the time goes in v4:
time: 332 us; the launch traced here: 331 us
  Pallas kernels  330 us (99%)
    pallas_call x1, Pallas kernels, front(): pl.pallas_call(front_kernel, name='front', out_shape=(jax.ShapeDtypeStruc...  190 us
    pallas_call x1, Pallas kernels, back(): pl.pallas_call(back_kernel, name='back', out_shape=(jax.ShapeDtypeStruct(...  130 us
    pallas_call x1, Pallas kernels, finish(): pl.pallas_call(finish_kernel, name='finish', out_shape=(f32(seq, width),...  10.3 us

profile of v4, /device:TPU:0, one launch (start us, length us, event | category | flops | bytes accessed | tf_op | source)
XLA Modules:
  0.0 331.2 jit_solution(7849781534733770373)
XLA Ops:
  0.6 189.7 %front.1 = (bf16[2048,1280]{1,0:T(8,128)(2,1)}, bf16[1024,2048]{1,0:T(8,128)(2,1)}, bf16[16,2048]{1,0:T(8,128)(2,1)}, bf16[176,2048]{1,0:T(8,128)(2,1)}, bf16[17...) custom-call(f32[176,2048]{1,0:T(8,128)} %resid_h.3, ...), custom_call_target="tpu_custom_call" | custom-call | tf_op jit(solution)/shard_map/front/pallas_call | solution.py:947
  190.4 130.3 %back.1 = (bf16[176,2048]{1,0:T(8,128)(2,1)}, f32[176,2048]{1,0:T(8,128)}, bf16[3,2816,128]{2,1,0:T(8,128)(2,1)}, bf16[128,1280]{1,0:T(8,128)(2,1)}, bf16[1024,128]{1,0:T(8,128)(2,1)}, /*index=5*/f32[8,128]{1,0:T(8,128)}) custom-call(bf16[704,2048]{1,0:T(8,128)(2,1)} %get-tuple-element.43.feed_p, bf16[3,704,2048]{2,1,0:T(8,128)(2,1)} %get-tuple-element.44.g3_p, ...), custom_call_target="tpu_custom_call" | custom-call | tf_op jit(solution)/shard_map/back/pallas_call | solution.py:1365
  320.7 10.3 %finish.1 = (f32[176,2048]{1,0:T(8,128)}, f32[176,2048]{1,0:T(8,128)}, f32[1,128,2816]{2,1,0:T(8,128)}, f32[1,128,2816]{2,1,0:T(8,128)}, f32[1,2816,128]{2,1,0:T...) custom-call(f32[176,2048]{1,0:T(8,128)} %get-tuple-element.42.mid_h,, ...), custom_call_target="tpu_custom_call" | custom-call | tf_op jit(solution)/shard_map/finish/pallas_call | solution.py:1499
